TPU v7x, 128 devices: a whole 4x4x4 slice. The times are simulated.
128 devices in a mesh: dom: 16 (over z, y), cls: 8 (over x, core).
Axes of the slice: x: 4, y: 4, z: 4, core: 2. Of those that a mesh axis runs over, the one named last changes fastest.
Arguments:
- images: bfloat16 [16384, 2, 16384], P(('dom', 'cls')), may hold values from -6 to 6
- slices: bfloat16 [128, 4, 2, 16384], P(('dom', 'cls')), may hold values from -6 to 6
- classes: int32 [16384], P(('dom', 'cls')), may hold values from 0 to 127, as said below
- rotations: int32 [16384], P(('dom', 'cls')), may hold values from 0 to 3
- defocus: int32 [16384], P(('dom', 'cls')), may hold values from 8000 to 29999
- groups: int32 [16384], P(('dom', 'cls')), may hold values from 0 to 1023, as said below
Outputs:
- sigma: float32 [1024, 64], P(('dom', 'cls'))
Inputs may be any that keep to these rules, and one draw needn't show every extreme that they name: Class c is owned by device c // 1 of dom+cls. In the rows of one device, at most 2 particles have classes of one owner; in every draw one owner gets exactly 2 from the rows of every device. `groups`: group g is owned by device g // 8 of dom+cls. Every group holds at least 8 particles.
All inputs are finite; a program needn't handle non-finite values.
Results may differ from a plain program's by a relative error of at most 0.0003.
Values may be sent and summed in bfloat16 or wider, within the bound.
No kernel may reach another device: no remote copies, remote signals or barrier semaphores. Data moves between devices by JAX's collectives and lax.ppermute only.
A program may use at most 192 MiB of HBM per device.

v0:
```python
import functools
import math

import jax
import jax.numpy as jnp
import numpy as np
from jax import lax
from jax.experimental import pallas as pl
from jax.experimental.pallas import tpu as pltpu
from jax.sharding import Mesh
from jax.sharding import PartitionSpec as P


AXES = ("z", "y", "x", "c")
RING = 4
SIDE = 128
HALF = SIDE // 2
SHELLS = 64
ROT = 4
P_DEV = 128
GROUPS_DEV = 8
DEVICES = 128
GROUPS = GROUPS_DEV * DEVICES
CANDIDATES = 2 * P_DEV

PIXEL_SIZE = 1.5
WAVELENGTH = 0.0197
SPHERICAL = 27000000.0
AMPLITUDE = 0.1

ROWS = 2 * SIDE
ROWS_A = 176
ROWS_B = ROWS - ROWS_A
RINGS_A = (("y", "z", "x"), ("x", "y", "z"))
RINGS_B = (("x", "z", "y"), ("z", "x", "y"))

DEPTH = 32
PACK = 4
STEP = 2 * PACK
RESULTS = CANDIDATES + STEP
A_ENDS, B_ENDS, IMAGE_AT = 16, 32, 48
A_LIST, B_LIST, DEPTH_AT = IMAGE_AT + RESULTS, IMAGE_AT + 2 * RESULTS, IMAGE_AT + 3 * RESULTS
LENGTHS = (16, 16, 16, 8, 8) + 3 * (16, 32, 16)
ALL = tuple(range(len(LENGTHS)))
EARLY = tuple(b for b in ALL if b not in (8, 9, 10))
SPAN = 64
NOWHERE = 127


def sine_terms():
    turns = np.cos(np.linspace(0, np.pi, 4001)) * 0.5
    turns = turns[np.abs(turns) > 1e-9]
    basis = np.stack([np.abs(turns) * turns ** (2 * k) for k in range(6)], 1)
    target = np.sin(2 * np.pi * turns) / turns * np.abs(turns)
    return [float(c) for c in np.linalg.lstsq(basis, target, rcond=None)[0]]


SINE = sine_terms()


def frequencies():
    offsets = np.arange(SIDE)
    return np.where(offsets < SIDE // 2, offsets, offsets - SIDE)


def tables():
    freq = frequencies()
    radius_sq = (freq[:, None] ** 2 + freq[None, :] ** 2).astype(np.float64)
    spatial = radius_sq / (SIDE * PIXEL_SIZE) ** 2
    rate = 0.5 * WAVELENGTH * spatial
    shift = -0.25 * SPHERICAL * WAVELENGTH**3 * spatial**2 + math.asin(AMPLITUDE) / (2 * math.pi)
    within = np.zeros((SIDE, 128), np.float32)
    for w in range(SIDE // 2 + 1):
        within[:, w] = np.abs(freq) <= w
    reach = np.full((HALF + 8, 128), NOWHERE, np.int32)
    for a in range(HALF + 1):
        for s in range(SHELLS):
            left = (s + 1) ** 2 - 1 - int(freq[a]) ** 2
            if left >= 0:
                reach[a, s] = min(math.isqrt(left), SIDE // 2)
    half = HALF + 8
    return (
        rate[:half].astype(np.float32),
        shift[:half].astype(np.float32),
        np.concatenate([within, within], 0),
        reach,
    )


def shell_pixels():
    freq = frequencies()
    radius_sq = freq[:, None] ** 2 + freq[None, :] ** 2
    return np.array(
        [((s * s <= radius_sq) & (radius_sq < (s + 1) ** 2)).sum() for s in range(SHELLS)], np.float32
    )


def shell_kernel(
    plan_ref, *refs, held, first,
):
    done, refs = (None, refs) if first else (refs[0], refs[1:])
    own, other, *refs = refs
    pieces = len(held[0]) + len(held[1])
    slices_a, slices_b = refs[: len(held[0])], refs[len(held[0]) : pieces]
    constants, (out, *scratch) = refs[pieces : pieces + 4], refs[pieces + 4 :]
    tables_here, (image, fetched, square, terms, image_sem, slice_sem, table_sem) = scratch[:4], scratch[4:]
    rate, shift, within, reach = tables_here
    begin, total = plan_ref[0], plan_ref[1]

    def table_copies():
        return [
            pltpu.make_async_copy(there, here, table_sem.at[i])
            for i, (there, here) in enumerate(zip(constants, tables_here))
        ]

    def fetch_slices(places, ends, numbers, parts, rows):
        for b, part in zip(numbers, parts):
            low, high = plan_ref[ends + b], plan_ref[ends + b + 1]

            def fetch(t, part=part):
                entry = plan_ref[places + t]
                j, at = entry // SPAN, entry % SPAN
                pltpu.make_async_copy(part.at[at], fetched.at[j, rows], slice_sem.at[j // STEP]).start()

            def fetch_some(i, carry, fetch=fetch, low=low):
                for k in range(4):
                    fetch(low + 4 * i + k)
                return carry

            def fetch_one(t, carry, fetch=fetch):
                fetch(t)
                return carry

            fours = (high - low) // 4
            lax.fori_loop(0, fours, fetch_some, 0)
            lax.fori_loop(low + 4 * fours, high, fetch_one, 0)

    def start(j, slot):
        at = plan_ref[IMAGE_AT + j]

        @pl.when(at < P_DEV)
        def _():
            pltpu.make_async_copy(own.at[at], image.at[slot], image_sem.at[slot]).start()

        @pl.when(at >= P_DEV)
        def _():
            pltpu.make_async_copy(other.at[at - P_DEV], image.at[slot], image_sem.at[slot]).start()

    def wait(slot):
        pltpu.make_async_copy(own.at[0], image.at[slot], image_sem.at[slot]).wait()

    for copy in table_copies():
        copy.start()

    def start_early(j, carry):
        start(j, lax.rem(j, DEPTH))
        return carry

    lax.fori_loop(begin, jnp.minimum(begin + DEPTH, total), start_early, 0)
    fetch_slices(A_LIST, A_ENDS, held[0], slices_a, pl.ds(0, ROWS_A))
    fetch_slices(B_LIST, B_ENDS, held[1], slices_b, pl.ds(ROWS_A, ROWS_B))
    sublane = lax.broadcasted_iota(jnp.int32, (8, 128), 0)
    out[...] = jnp.zeros_like(out) if first else done[...]
    half, top = sublane // 2, sublane == 0
    back = jnp.where(top, 0, 8 - sublane)
    first = half == 0
    low, high, zero, down = half, half + 4, half * 0, 4 - half
    wrap = jnp.where(first, 0, 8 - half)

    def rows_of(v, index):
        return jnp.take_along_axis(v, index, axis=0, mode="promise_in_bounds")

    def waves(j):
        depth = plan_ref[DEPTH_AT + j].astype(jnp.float32)
        result = []
        for g in range(SIDE // 16 + 1):
            turns = depth * rate[8 * g : 8 * g + 8, :] + shift[8 * g : 8 * g + 8, :]
            turns = turns - jnp.round(turns)
            sq = turns * turns
            y = sq * SINE[-1] + SINE[-2]
            for term in SINE[-3::-1]:
                y = y * sq + term
            result.append(y * turns)
        return result

    def spread(s, v):
        if v < 16:
            return rows_of(s[v // 2], high if v % 2 else low)
        h = v - 16
        if h % 2:
            return rows_of(s[(15 - h) // 2], down)
        m = 8 - h // 2
        return jnp.where(first, rows_of(s[m], zero), rows_of(s[m - 1], wrap))

    def keep(k, at, pair):
        p = jnp.concatenate(pair, 0)
        high_part = p.astype(jnp.bfloat16)
        terms[k, at : at + 16, 0:128] = high_part
        terms[k, at : at + 16, 128:256] = (p - high_part.astype(jnp.float32)).astype(jnp.bfloat16)

    def power(j, slot, k, m):
        s = waves(j)

        def pixel_power(g):
            for h in range(2):
                v = 4 * g + 2 * h
                r = pl.ds(8 * v, 16)
                wave = jnp.concatenate([spread(s, v), spread(s, v + 1)], 0)
                e = image[slot, r, :].astype(jnp.float32) + wave * fetched[j, r, :].astype(jnp.float32)
                square[m % 2, r, :] = e * e
            both = [square[m % 2, pl.ds(32 * g + part, 16, stride=2), :] for part in range(2)]
            p = both[0] + both[1]
            return [p[:8], p[8:]]

        turned = [rows_of(p, back) for g in range(4, 8) for p in pixel_power(g)]
        turned.append(jnp.zeros((8, 128), jnp.float32))
        for g in range(4):
            near = pixel_power(g)
            for h in range(2):
                v = 2 * g + h
                near[h] = near[h] + jnp.where(top, turned[8 - v], turned[7 - v])
            keep(k, HALF * m + 16 * g, near)
        return jnp.where(top, turned[0], 0.0)

    def keep_edges(edges, k):
        for at in range(0, PACK, 2):
            keep(k, HALF * PACK + 8 * at, edges[at : at + 2])

    def collect(sums, j, m):
        parts = [jnp.zeros((8, 128), jnp.float32) for _ in range(2)]
        starts = [HALF * m + 8 * g for g in range(8)] + [HALF * PACK + 8 * m]
        for g, at in enumerate(starts):
            index = reach[8 * g : 8 * g + 8, :]
            found = jnp.take_along_axis(sums[at : at + 8], index, axis=1, mode="promise_in_bounds")
            parts[g % 2] = parts[g % 2] + found
        out[pl.ds(j, 1), :] = jnp.sum(parts[0] + parts[1], axis=0, keepdims=True)

    def region(j, slot, k, before):
        sums = jnp.dot(terms[1 - k], within[...], preferred_element_type=jnp.float32)
        edges = []
        for m in range(PACK):
            edges.append(power(j + m, slot + m, k, m))
            collect(sums, before + m, m)
        keep_edges(edges, k)

    def step(i, carry):
        j = STEP * i
        slot = lax.rem(j, DEPTH)
        block = fetched.at[pl.ds(j, STEP)]
        pltpu.make_async_copy(own.at[pl.ds(0, STEP)], block, slice_sem.at[i]).wait()
        for m in range(STEP):
            wait(slot + m)
        region(j, slot, 0, jnp.maximum(j - PACK, begin))
        region(j + PACK, slot + PACK, 1, j)
        for m in range(STEP):

            @pl.when(j + m + DEPTH < total)
            def _(m=m):
                start(j + m + DEPTH, slot + m)

        return carry

    terms[...] = jnp.zeros_like(terms)
    for copy in table_copies():
        copy.wait()
    lax.fori_loop(begin // STEP, total // STEP, step, 0)

    @pl.when(total > begin)
    def _():
        sums = jnp.dot(terms[1], within[...], preferred_element_type=jnp.float32)
        for m in range(PACK):
            collect(sums, total - PACK + m, m)


def shell_sums(held, plan, done, own, other, slices_a, slices_b):
    before = () if done is None else (done,)
    rate, shift, within, reach = tables()
    constants = jnp.asarray(rate), jnp.asarray(shift), jnp.asarray(within, jnp.bfloat16), jnp.asarray(reach)
    smem = pl.BlockSpec(memory_space=pltpu.SMEM)
    hbm = pl.BlockSpec(memory_space=pltpu.HBM)
    vmem = pl.BlockSpec(memory_space=pltpu.VMEM)
    return pl.pallas_call(
        functools.partial(shell_kernel, held=held, first=done is None),
        out_shape=jax.ShapeDtypeStruct((RESULTS, 128), jnp.float32),
        in_specs=[smem] + [vmem] * len(before) + [hbm] * (2 + len(held[0]) + len(held[1]) + len(constants)),
        out_specs=vmem,
        scratch_shapes=[
            *(pltpu.VMEM(c.shape, c.dtype) for c in constants),
            pltpu.VMEM((DEPTH, ROWS, 128), jnp.bfloat16),
            pltpu.VMEM((RESULTS, ROWS, 128), jnp.bfloat16),
            pltpu.VMEM((2, ROWS, 128), jnp.float32),
            pltpu.VMEM((2, (HALF + 8) * PACK, 256), jnp.bfloat16),
            pltpu.SemaphoreType.DMA((DEPTH,)),
            pltpu.SemaphoreType.DMA((RESULTS // STEP,)),
            pltpu.SemaphoreType.DMA((len(constants),)),
        ],
    )(
        plan, *before, own, other,
        *(slices_a[b] for b in held[0]), *(slices_b[b] for b in held[1]), *constants,
    )


def ring_pairs(rings, step):
    pairs = []
    for source in range(DEVICES):
        at = {"z": source // 32, "y": source // 8 % 4, "x": source // 2 % 4, "c": source % 2}
        to = dict(at)
        ring = rings[at["c"]]
        to[ring] = (at[ring] + step) % RING
        pairs.append((source, ((to["z"] * 4 + to["y"]) * 4 + to["x"]) * 2 + to["c"]))
    return pairs


def send(x, rings, step):
    return lax.ppermute(x, AXES, ring_pairs(rings, step))


def joined(parts):
    return jnp.concatenate(parts, 0)


def last_ring(own, near, rest, rings):
    parts = own, near, rest
    left = [send(x, rings, 1) for x in parts]
    right = [send(x, rings, -1) for x in parts]
    far = (send(right[0], rings, -1), send(left[1], rings, 1), send(right[2], rings, -1))
    return (*right, *far, *left)


def gather_part(x, rings):
    first, second, third = zip(*rings)
    x = x, send(x, first, -1), send(x, first, 2), send(x, first, 1)
    block = joined(x)
    half = block.shape[0] // 2
    right, left = send(block, second, -1), send(block, second, 1)
    far = send(left[:half], second, 1), send(right[half:], second, -1)
    near, rest = joined((right, left)), joined(far)
    return (block, right, left, *far, *last_ring(block, near, rest, third))


def place_of(owner, rotation, rings, core):
    here = {a: lax.axis_index(a) for a in AXES}
    ahead = {
        "z": (owner // 32 - here["z"]) % RING,
        "y": (owner // 8 % 4 - here["y"]) % RING,
        "x": (owner // 2 % 4 - here["x"]) % RING,
    }
    places = [
        ((ahead[r[2]] * 4 + (ahead[r[1]] ^ (ahead[r[1]] >> 1))) * 4 + ahead[r[0]]) * ROT + rotation for r in rings
    ]
    return jnp.where(core == 0, places[0], places[1])


def by_piece(place, here, wanted, index):
    starts = np.cumsum((0,) + LENGTHS)
    place = jnp.where(here, place, 0)
    piece = sum((place >= int(edge)).astype(jnp.int32) for edge in starts[1:-1])
    at = place - sum(jnp.where(piece == b, int(starts[b]), 0) for b in range(len(LENGTHS)))
    piece = jnp.where(wanted, piece, len(LENGTHS))
    key = piece * RESULTS + index
    rank = jnp.sum((key[None, :] < key[:, None]).astype(jnp.int32), axis=1)
    entry = index * SPAN + at
    places = jnp.sum(jnp.where(rank[None, :] == index[:, None], entry[None, :], 0), axis=1)
    edges = jnp.arange(16, dtype=jnp.int32)
    return places, jnp.sum((piece[None, :] < edges[:, None]).astype(jnp.int32), axis=1)


def swapped(x):
    return lax.ppermute(x, "c", [(0, 1), (1, 0)])


def by_rows(x):
    lead = x.shape[:-2]
    x = x.reshape(*lead, 2, SIDE, SIDE)
    return jnp.swapaxes(x, -3, -2).reshape(*lead, ROWS, SIDE)


def plan(facts, core):
    owner, rotation, depth, group = facts
    mine = owner % 2 == core
    a_place = place_of(owner, rotation, RINGS_A, core)
    b_place = place_of(owner, rotation, RINGS_B, core)
    late = mine & ((a_place // SPAN == 2) | (b_place // SPAN == 2))
    early = mine & ~late

    def ranks(mask):
        i = jnp.arange(CANDIDATES, dtype=jnp.int32)
        before = (i[None, :] < i[:, None]) & mask[None, :]
        return jnp.sum(before.astype(jnp.int32), axis=1), jnp.sum(mask.astype(jnp.int32))

    def whole_steps(n):
        return (n + STEP - 1) // STEP * STEP

    early_rank, early_count = ranks(early)
    late_rank, late_count = ranks(late)
    middle = whole_steps(early_count)
    end = middle + whole_steps(late_count)
    index = jnp.arange(RESULTS, dtype=jnp.int32)
    row = jnp.where(early, early_rank, jnp.where(late, middle + late_rank, -1))
    chosen = row[None, :] == index[:, None]

    def packed(values):
        return jnp.sum(jnp.where(chosen, values[None, :], 0), axis=1)

    depth = packed(depth)
    here = (index < early_count) | ((index >= middle) & (index < middle + late_count))
    group = jnp.where(here, packed(group), -1)
    image_at = packed(jnp.arange(CANDIDATES, dtype=jnp.int32))
    a_place, b_place = packed(a_place), packed(b_place)
    plans = []
    for begin, until in ((jnp.int32(0), middle), (middle, end)):
        wanted = (index >= begin) & (index < until)
        a_list, a_ends = by_piece(a_place, here, wanted, index)
        b_list, b_ends = by_piece(b_place, here, wanted, index)
        head = jnp.arange(16, dtype=jnp.int32)
        span = jnp.where(head == 0, begin, until)
        plans.append(jnp.concatenate([span, a_ends, b_ends, image_at, a_list, b_list, depth]))
    return group, plans


def body(images, slices, classes, rotations, defocus, groups):
    core = lax.axis_index("c")
    facts = jnp.stack([classes, rotations, defocus, groups])
    facts = jnp.concatenate([facts, swapped(facts)], 1)
    own = by_rows(images)
    other = swapped(own)
    own_slices = by_rows(slices[0])
    slices_a = gather_part(own_slices[:, :ROWS_A], RINGS_A)
    slices_b = gather_part(own_slices[:, ROWS_A:], RINGS_B)
    group, plans = plan(facts, core)
    sums = None
    for held, one in (((EARLY, EARLY), plans[0]), ((ALL, ALL), plans[1])):
        sums = shell_sums(held, one, sums, own, other, slices_a, slices_b)
    lane = jnp.arange(128, dtype=jnp.int32)
    inner = jnp.pad(sums[:, : SHELLS - 1], ((0, 0), (1, 128 - SHELLS)))
    sums = jnp.where(lane < SHELLS, sums - inner, jnp.where(lane == SHELLS, 1.0, 0.0))
    high = lax.reduce_precision(sums, 8, 7)
    parts = jnp.concatenate([high, sums - high], 1).astype(jnp.bfloat16)
    member = (jnp.arange(GROUPS, dtype=jnp.int32)[:, None] == group[None, :]).astype(jnp.bfloat16)
    partial = jnp.dot(member, parts, preferred_element_type=jnp.float32)
    partial = partial[:, :128] + partial[:, 128:]
    arrived = lax.all_to_all(partial.reshape(DEVICES, GROUPS_DEV, 128), AXES, 0, 0, tiled=True)
    own_groups = jnp.sum(arrived, axis=0)
    return own_groups[:, :SHELLS] / (2.0 * own_groups[:, SHELLS : SHELLS + 1] * jnp.asarray(shell_pixels()))


def solution(mesh):
    finer = Mesh(mesh.devices.reshape(4, 4, 4, 2), AXES)
    placed = (
        P(AXES, None, None),
        P(AXES, None, None, None),
        P(AXES),
        P(AXES),
        P(AXES),
        P(AXES),
    )
    return jax.shard_map(body, mesh=finer, in_specs=placed, out_specs=P(AXES, None), check_vma=False)
```

profile of v0, /device:TPU:0, one launch (start us, length us, event | category | flops | bytes accessed | tf_op | source)
XLA Modules:
  0.0 160.4 jit_solution(12695038788300448289)
XLA Ops:
  0.9 2.9 %collective-permute-start.15 = (bf16[4,80,128]{2,1,0:T(8,128)(2,1)S(1)}, bf16[4,80,128]{2,1,0:T(8,128)(2,1)S(1)}, u32[]{:S(2)}, u32[]{:S(2)}) collective-permute-start(bf16[4,80,128]{2,1,0:T(8,128)(2,1)S(1)} %slice.47), channel_id=1, source_target_pairs={{0,6},{1,97},{2,0},{3,99},{4,2},{5,101},{6,4},{7,103},{8,14},{9,10... | collective-permute-start | bytes 245768 | tf_op jit(solution)/shard_map/ppermute | solution.py:315
  6.4 3.1 %collective-permute-start.2 = (bf16[4,176,128]{2,1,0:T(8,128)(2,1)S(1)}, bf16[4,176,128]{2,1,0:T(8,128)(2,1)S(1)}, u32[]{:S(2)}, u32[]{:S(2)}) collective-permute-start(bf16[4,176,128]{2,1,0:T(8,128)(2,1)S(1)} %slice.44), channel_id=1, source_target_pairs={{0,24},{1,7},{2,26},{3,1},{4,28},{5,3},{6,30},{7,5},{8,0},{9,15},{... | collective-permute-start | bytes 540680 | tf_op jit(solution)/shard_map/ppermute | solution.py:315
  12.0 1.5 collective-permute-done
  13.5 2.0 %collective-permute-start.19 = (bf16[16,80,128]{2,1,0:T(8,128)(2,1)S(1)}, bf16[16,80,128]{2,1,0:T(8,128)(2,1)S(1)}, u32[]{:S(2)}, u32[]{:S(2)}) collective-permute-start(bf16[16,80,128]{2,1,0:T(8,128)(2,1)S(1)} %pad_maximum_fusion.1.refs_13_.refs_17_), channel_id=1, source_target_pairs={{0,32},{1,3},{2,34},{3,5},{4,36},{5,7},{6,38},{7,1},{8,40},{9,11},... | collective-permute-start | bytes 983048 | tf_op jit(solution)/shard_map/ppermute | solution.py:315
  16.3 2.2 %collective-permute-start.18 = (bf16[16,80,128]{2,1,0:T(8,128)(2,1)S(1)}, bf16[16,80,128]{2,1,0:T(8,128)(2,1)S(1)}, u32[]{:S(2)}, u32[]{:S(2)}) collective-permute-start(bf16[16,80,128]{2,1,0:T(8,128)(2,1)S(1)} %pad_maximum_fusion.1.refs_13_.refs_17_), channel_id=1, source_target_pairs={{0,96},{1,7},{2,98},{3,1},{4,100},{5,3},{6,102},{7,5},{8,104},{9,1... | collective-permute-start | bytes 983048 | tf_op jit(solution)/shard_map/ppermute | solution.py:315
  18.4 3.0 %collective-permute-start.22 = (bf16[16,80,128]{2,1,0:T(8,128)(2,1)S(1)}, bf16[16,80,128]{2,1,0:T(8,128)(2,1)}, u32[]{:S(2)}, u32[]{:S(2)}) collective-permute-start(bf16[16,80,128]{2,1,0:T(8,128)(2,1)S(1)} %pad_maximum_fusion.1.refs_13_.refs_17_), channel_id=1, source_target_pairs={{0,24},{1,25},{2,26},{3,27},{4,28},{5,29},{6,30},{7,31},{8,0},{9,1... | collective-permute-start | bytes 983048 | tf_op jit(solution)/shard_map/ppermute | solution.py:315
  22.7 2.2 %collective-permute-start.5 = (bf16[16,176,128]{2,1,0:T(8,128)(2,1)S(1)}, bf16[16,176,128]{2,1,0:T(8,128)(2,1)S(1)}, u32[]{:S(2)}, u32[]{:S(2)}) collective-permute-start(bf16[16,176,128]{2,1,0:T(8,128)(2,1)S(1)} %pad_maximum_fusion.refs_2_.refs_3_), channel_id=1, source_target_pairs={{0,96},{1,25},{2,98},{3,27},{4,100},{5,29},{6,102},{7,31},{8,104},... | collective-permute-start | bytes 2162696 | tf_op jit(solution)/shard_map/ppermute | solution.py:315
  25.3 4.2 %collective-permute-done.22.refs_18_.refs_22_ = bf16[16,80,128]{2,1,0:T(8,128)(2,1)} collective-permute-done((bf16[16,80,128]{2,1,0:T(8,128)(2,1)S(1)}, bf16[16,80,128]{2,1,0:T(8,128)(2,1)}, u32[]{:S(2)}, u32[]{:S(2)}) %collective-permute-start.22) | collective-permute-done | bytes 327712 | tf_op jit(solution)/shard_map/ppermute | solution.py:315
  29.6 2.5 %collective-permute-start.21 = (bf16[8,80,128]{2,1,0:T(8,128)(2,1)S(1)}, bf16[8,80,128]{2,1,0:T(8,128)(2,1)S(1)}, u32[]{:S(2)}, u32[]{:S(2)}) collective-permute-start(bf16[8,80,128]{2,1,0:T(8,128)(2,1)S(1)} %slice.49), channel_id=1, source_target_pairs={{0,96},{1,7},{2,98},{3,1},{4,100},{5,3},{6,102},{7,5},{8,104},{9,1... | collective-permute-start | bytes 491528 | tf_op jit(solution)/shard_map/ppermute | solution.py:315
  32.2 3.7 %collective-permute-done.20.refs_16_.refs_20_ = bf16[8,80,128]{2,1,0:T(8,128)(2,1)S(1)} collective-permute-done((bf16[8,80,128]{2,1,0:T(8,128)(2,1)S(1)}, bf16[8,80,128]{2,1,0:T(8,128)(2,1)S(1)}, u32[]{:S(2)}, u32[]{:S(2)}) %collective-permute-start.20) | collective-permute-done | bytes 163872 | tf_op jit(solution)/shard_map/ppermute | solution.py:315
  35.9 3.2 %collective-permute-start.31 = (bf16[16,80,128]{2,1,0:T(8,128)(2,1)}, bf16[16,80,128]{2,1,0:T(8,128)(2,1)}, u32[]{:S(2)}, u32[]{:S(2)}) collective-permute-start(bf16[16,80,128]{2,1,0:T(8,128)(2,1)} %collective-permute-done.22.refs_18_.refs_22_), channel_id=1, source_target_pairs={{0,24},{1,25},{2,26},{3,27},{4,28},{5,29},{6,30},{7,31},{8,0},{9,1... | collective-permute-start | bytes 983048 | tf_op jit(solution)/shard_map/ppermute | solution.py:315
  40.7 4.7 %collective-permute-done.25.refs_21_.refs_28_ = bf16[16,80,128]{2,1,0:T(8,128)(2,1)} collective-permute-done((bf16[16,80,128]{2,1,0:T(8,128)(2,1)S(1)}, bf16[16,80,128]{2,1,0:T(8,128)(2,1)}, u32[]{:S(2)}, u32[]{:S(2)}) %collective-permute-start.25) | collective-permute-done | bytes 327712 | tf_op jit(solution)/shard_map/ppermute | solution.py:315
  47.6 4.0 %collective-permute-start.9 = (bf16[16,176,128]{2,1,0:T(8,128)(2,1)S(1)}, bf16[16,176,128]{2,1,0:T(8,128)(2,1)S(1)}, u32[]{:S(2)}, u32[]{:S(2)}) collective-permute-start(bf16[16,176,128]{2,1,0:T(8,128)(2,1)S(1)} %pad_maximum_fusion.refs_2_.refs_3_), channel_id=1, source_target_pairs={{0,6},{1,97},{2,0},{3,99},{4,2},{5,101},{6,4},{7,103},{8,14},{9,10... | collective-permute-start | bytes 2162696 | tf_op jit(solution)/shard_map/ppermute | solution.py:315
  53.7 4.5 %collective-permute-done.27.refs_23_.refs_30_ = bf16[16,80,128]{2,1,0:T(8,128)(2,1)S(1)} collective-permute-done((bf16[16,80,128]{2,1,0:T(8,128)(2,1)S(1)}, bf16[16,80,128]{2,1,0:T(8,128)(2,1)S(1)}, u32[]{:S(2)}, u32[]{:S(2)}) %collective-permute-start.27) | collective-permute-done | bytes 327712 | tf_op jit(solution)/shard_map/ppermute | solution.py:315
  60.4 3.7 %collective-permute-done.12.refs_10_.refs_14_ = bf16[16,176,128]{2,1,0:T(8,128)(2,1)S(1)} collective-permute-done((bf16[16,176,128]{2,1,0:T(8,128)(2,1)S(1)}, bf16[16,176,128]{2,1,0:T(8,128)(2,1)S(1)}, u32[]{:S(2)}, u32[]{:S(2)}) %collective-permute-start.12) | collective-permute-done | bytes 720928 | tf_op jit(solution)/shard_map/ppermute | solution.py:315
  66.2 2.4 %collective-permute-start.8 = (bf16[8,176,128]{2,1,0:T(8,128)(2,1)S(1)}, bf16[8,176,128]{2,1,0:T(8,128)(2,1)S(1)}, u32[]{:S(2)}, u32[]{:S(2)}) collective-permute-start(bf16[8,176,128]{2,1,0:T(8,128)(2,1)S(1)} %slice.46), channel_id=1, source_target_pairs={{0,96},{1,25},{2,98},{3,27},{4,100},{5,29},{6,102},{7,31},{8,104},... | collective-permute-start | bytes 1081352 | tf_op jit(solution)/shard_map/ppermute | solution.py:315
  70.4 3.2 %collective-permute-done.8.refs_6_.refs_7_ = bf16[8,176,128]{2,1,0:T(8,128)(2,1)S(1)} collective-permute-done((bf16[8,176,128]{2,1,0:T(8,128)(2,1)S(1)}, bf16[8,176,128]{2,1,0:T(8,128)(2,1)S(1)}, u32[]{:S(2)}, u32[]{:S(2)}) %collective-permute-start.8) | collective-permute-done | bytes 360480 | tf_op jit(solution)/shard_map/ppermute | solution.py:315
  73.6 3.4 %collective-permute-start.10 = (bf16[32,176,128]{2,1,0:T(8,128)(2,1)}, bf16[32,176,128]{2,1,0:T(8,128)(2,1)S(1)}, u32[]{:S(2)}, u32[]{:S(2)}) collective-permute-start(bf16[32,176,128]{2,1,0:T(8,128)(2,1)} %constant_dynamic-update-slice_fusion), channel_id=1, source_target_pairs={{0,6},{1,97},{2,0},{3,99},{4,2},{5,101},{6,4},{7,103},{8,14},{9,10... | collective-permute-start | bytes 4325384 | tf_op jit(solution)/shard_map/ppermute | solution.py:315
  80.9 20.5 %collective-permute-done.11.refs_9_.refs_10_ = bf16[16,176,128]{2,1,0:T(8,128)(2,1)} collective-permute-done((bf16[16,176,128]{2,1,0:T(8,128)(2,1)S(1)}, bf16[16,176,128]{2,1,0:T(8,128)(2,1)}, u32[]{:S(2)}, u32[]{:S(2)}) %collective-permute-start.11) | collective-permute-done | bytes 720928 | tf_op jit(solution)/shard_map/ppermute | solution.py:315
  101.4 3.8 %collective-permute-start.28 = (bf16[16,176,128]{2,1,0:T(8,128)(2,1)S(1)}, bf16[16,176,128]{2,1,0:T(8,128)(2,1)}, u32[]{:S(2)}, u32[]{:S(2)}) collective-permute-start(bf16[16,176,128]{2,1,0:T(8,128)(2,1)S(1)} %copy-done.10), channel_id=1, source_target_pairs={{0,6},{1,97},{2,0},{3,99},{4,2},{5,101},{6,4},{7,103},{8,14},{9,10... | collective-permute-start | bytes 2162696 | tf_op jit(solution)/shard_map/ppermute | solution.py:315
  106.6 3.3 %collective-permute-start.33 = (bf16[16,80,128]{2,1,0:T(8,128)(2,1)S(1)}, bf16[16,80,128]{2,1,0:T(8,128)(2,1)}, u32[]{:S(2)}, u32[]{:S(2)}) collective-permute-start(bf16[16,80,128]{2,1,0:T(8,128)(2,1)S(1)} %copy-done.16), channel_id=1, source_target_pairs={{0,24},{1,25},{2,26},{3,27},{4,28},{5,29},{6,30},{7,31},{8,0},{9,1... | collective-permute-start | bytes 983048 | tf_op jit(solution)/shard_map/ppermute | solution.py:315
  111.4 13.5 %shard_map.145.refs_0_ = f32[264,128]{1,0:T(8,128)} custom-call(s32[1104]{0:T(1024)} %concatenate.33.plan_ref, bf16[128,256,128]{2,1,0:T(8,128)(2,1)} %bitcast.27, bf16[128,256,128]{2,1,0:T(8,128)(2,1)} %collective-permute-done.1.refs_1_.refs_2_, bf16[16,176,128]{2,1,0:T(8,128)(2,1)} %copy-done.2, bf16[16,176,128]{2,1,0:T(8,128)(2,1)} %copy-done.1, ...), custom_call_target="tpu_custom_call" | custom-call | tf_op jit(solution)/shard_map/pallas_call | solution.py:282
  125.0 10.7 %shard_map.146 = f32[264,128]{1,0:T(8,128)} custom-call(s32[1104]{0:T(1024)} %concatenate.32.plan_ref, f32[264,128]{1,0:T(8,128)} %shard_map.145.refs_0_, bf16[128,256,128]{2,1,0:T(8,128)(2,1)} %bitcast.28, bf16[128,256,128]{2,1,0:T(8,128)(2,1)} %collective-permute-done.1.refs_1_.refs_2_, bf16[16,176,128]{2,1,0:T(8,128)(2,1)} %copy-done.2, ...), custom_call_target="tpu_custom_call" | custom-call | tf_op jit(solution)/shard_map/pallas_call | solution.py:282
  137.3 22.1 %all_to_all.5 = f32[128,8,128]{2,1,0:T(8,128)S(1)} all-to-all(f32[128,8,128]{2,1,0:T(8,128)S(1)} %fusion.2), channel_id=1, replica_groups=mesh['z'=4,'y'=4,'x'=4,'c'=2] {'z','y','x','c'}, dimensions={0} | all-to-all | bytes 1048576 | tf_op jit(solution)/shard_map/all_to_all | solution.py:442
  (135 shorter events, 27.4 us)
Async XLA Ops:
  0.0 106.6 %collective-permute-start.1 = (bf16[128,256,128]{2,1,0:T(8,128)(2,1)}, bf16[128,256,128]{2,1,0:T(8,128)(2,1)}, u32[]{:S(2)}, u32[]{:S(2)}) collective-permute-start(bf16[128,256,128]{2,1,0:T(8,128)(2,1)} %bitcast.26), channel_id=1, source_target_pairs={{0,1},{1,0},{2,3},{3,2},{4,5},{5,4},{6,7},{7,6},{8,9},{9,8},{10,11... | collective-permute-start | bytes 25165832 | tf_op jit(solution)/shard_map/ppermute | solution.py:369
  6.4 9.9 %collective-permute-start.2 = (bf16[4,176,128]{2,1,0:T(8,128)(2,1)S(1)}, bf16[4,176,128]{2,1,0:T(8,128)(2,1)S(1)}, u32[]{:S(2)}, u32[]{:S(2)}) collective-permute-start(bf16[4,176,128]{2,1,0:T(8,128)(2,1)S(1)} %slice.44), channel_id=1, source_target_pairs={{0,24},{1,7},{2,26},{3,1},{4,28},{5,3},{6,30},{7,5},{8,0},{9,15},{... | collective-permute-start | bytes 540680 | tf_op jit(solution)/shard_map/ppermute | solution.py:315
  10.9 10.6 %collective-permute-start.4 = (bf16[4,176,128]{2,1,0:T(8,128)(2,1)S(1)}, bf16[4,176,128]{2,1,0:T(8,128)(2,1)S(1)}, u32[]{:S(2)}, u32[]{:S(2)}) collective-permute-start(bf16[4,176,128]{2,1,0:T(8,128)(2,1)S(1)} %slice.44), channel_id=1, source_target_pairs={{0,8},{1,3},{2,10},{3,5},{4,12},{5,7},{6,14},{7,1},{8,16},{9,11},{... | collective-permute-start | bytes 540680 | tf_op jit(solution)/shard_map/ppermute | solution.py:315
  18.4 11.1 %collective-permute-start.22 = (bf16[16,80,128]{2,1,0:T(8,128)(2,1)S(1)}, bf16[16,80,128]{2,1,0:T(8,128)(2,1)}, u32[]{:S(2)}, u32[]{:S(2)}) collective-permute-start(bf16[16,80,128]{2,1,0:T(8,128)(2,1)S(1)} %pad_maximum_fusion.1.refs_13_.refs_17_), channel_id=1, source_target_pairs={{0,24},{1,25},{2,26},{3,27},{4,28},{5,29},{6,30},{7,31},{8,0},{9,1... | collective-permute-start | bytes 983048 | tf_op jit(solution)/shard_map/ppermute | solution.py:315
  21.6 26.0 %collective-permute-start.6 = (bf16[16,176,128]{2,1,0:T(8,128)(2,1)S(1)}, bf16[16,176,128]{2,1,0:T(8,128)(2,1)S(1)}, u32[]{:S(2)}, u32[]{:S(2)}) collective-permute-start(bf16[16,176,128]{2,1,0:T(8,128)(2,1)S(1)} %pad_maximum_fusion.refs_2_.refs_3_), channel_id=1, source_target_pairs={{0,32},{1,9},{2,34},{3,11},{4,36},{5,13},{6,38},{7,15},{8,40},{9,1... | collective-permute-start | bytes 2162696 | tf_op jit(solution)/shard_map/ppermute | solution.py:315
  22.7 28.9 %collective-permute-start.5 = (bf16[16,176,128]{2,1,0:T(8,128)(2,1)S(1)}, bf16[16,176,128]{2,1,0:T(8,128)(2,1)S(1)}, u32[]{:S(2)}, u32[]{:S(2)}) collective-permute-start(bf16[16,176,128]{2,1,0:T(8,128)(2,1)S(1)} %pad_maximum_fusion.refs_2_.refs_3_), channel_id=1, source_target_pairs={{0,96},{1,25},{2,98},{3,27},{4,100},{5,29},{6,102},{7,31},{8,104},... | collective-permute-start | bytes 2162696 | tf_op jit(solution)/shard_map/ppermute | solution.py:315
  25.0 10.9 %collective-permute-start.20 = (bf16[8,80,128]{2,1,0:T(8,128)(2,1)S(1)}, bf16[8,80,128]{2,1,0:T(8,128)(2,1)S(1)}, u32[]{:S(2)}, u32[]{:S(2)}) collective-permute-start(bf16[8,80,128]{2,1,0:T(8,128)(2,1)S(1)} %slice.48), channel_id=1, source_target_pairs={{0,32},{1,3},{2,34},{3,5},{4,36},{5,7},{6,38},{7,1},{8,40},{9,11},... | collective-permute-start | bytes 491528 | tf_op jit(solution)/shard_map/ppermute | solution.py:315
  35.9 9.5 %collective-permute-start.25 = (bf16[16,80,128]{2,1,0:T(8,128)(2,1)S(1)}, bf16[16,80,128]{2,1,0:T(8,128)(2,1)}, u32[]{:S(2)}, u32[]{:S(2)}) collective-permute-start(bf16[16,80,128]{2,1,0:T(8,128)(2,1)S(1)} %pad_maximum_fusion.1.refs_13_.refs_17_), channel_id=1, source_target_pairs={{0,8},{1,9},{2,10},{3,11},{4,12},{5,13},{6,14},{7,15},{8,16},{9,17... | collective-permute-start | bytes 983048 | tf_op jit(solution)/shard_map/ppermute | solution.py:315
  35.9 10.5 %collective-permute-start.31 = (bf16[16,80,128]{2,1,0:T(8,128)(2,1)}, bf16[16,80,128]{2,1,0:T(8,128)(2,1)}, u32[]{:S(2)}, u32[]{:S(2)}) collective-permute-start(bf16[16,80,128]{2,1,0:T(8,128)(2,1)} %collective-permute-done.22.refs_18_.refs_22_), channel_id=1, source_target_pairs={{0,24},{1,25},{2,26},{3,27},{4,28},{5,29},{6,30},{7,31},{8,0},{9,1... | collective-permute-start | bytes 983048 | tf_op jit(solution)/shard_map/ppermute | solution.py:315
  46.4 11.8 %collective-permute-start.27 = (bf16[16,80,128]{2,1,0:T(8,128)(2,1)S(1)}, bf16[16,80,128]{2,1,0:T(8,128)(2,1)S(1)}, u32[]{:S(2)}, u32[]{:S(2)}) collective-permute-start(bf16[16,80,128]{2,1,0:T(8,128)(2,1)S(1)} %constant_dynamic-update-slice_fusion.6), channel_id=1, source_target_pairs={{0,8},{1,9},{2,10},{3,11},{4,12},{5,13},{6,14},{7,15},{8,16},{9,17... | collective-permute-start | bytes 983048 | tf_op jit(solution)/shard_map/ppermute | solution.py:315
  47.6 12.9 %collective-permute-start.9 = (bf16[16,176,128]{2,1,0:T(8,128)(2,1)S(1)}, bf16[16,176,128]{2,1,0:T(8,128)(2,1)S(1)}, u32[]{:S(2)}, u32[]{:S(2)}) collective-permute-start(bf16[16,176,128]{2,1,0:T(8,128)(2,1)S(1)} %pad_maximum_fusion.refs_2_.refs_3_), channel_id=1, source_target_pairs={{0,6},{1,97},{2,0},{3,99},{4,2},{5,101},{6,4},{7,103},{8,14},{9,10... | collective-permute-start | bytes 2162696 | tf_op jit(solution)/shard_map/ppermute | solution.py:315
  51.6 12.5 %collective-permute-start.12 = (bf16[16,176,128]{2,1,0:T(8,128)(2,1)S(1)}, bf16[16,176,128]{2,1,0:T(8,128)(2,1)S(1)}, u32[]{:S(2)}, u32[]{:S(2)}) collective-permute-start(bf16[16,176,128]{2,1,0:T(8,128)(2,1)S(1)} %pad_maximum_fusion.refs_2_.refs_3_), channel_id=1, source_target_pairs={{0,2},{1,33},{2,4},{3,35},{4,6},{5,37},{6,0},{7,39},{8,10},{9,41},... | collective-permute-start | bytes 2162696 | tf_op jit(solution)/shard_map/ppermute | solution.py:315
  53.6 12.6 %collective-permute-start.7 = (bf16[8,176,128]{2,1,0:T(8,128)(2,1)S(1)}, bf16[8,176,128]{2,1,0:T(8,128)(2,1)S(1)}, u32[]{:S(2)}, u32[]{:S(2)}) collective-permute-start(bf16[8,176,128]{2,1,0:T(8,128)(2,1)S(1)} %slice.45), channel_id=1, source_target_pairs={{0,32},{1,9},{2,34},{3,11},{4,36},{5,13},{6,38},{7,15},{8,40},{9,1... | collective-permute-start | bytes 1081352 | tf_op jit(solution)/shard_map/ppermute | solution.py:315
  58.2 21.7 %collective-permute-start.13 = (bf16[32,176,128]{2,1,0:T(8,128)(2,1)}, bf16[32,176,128]{2,1,0:T(8,128)(2,1)}, u32[]{:S(2)}, u32[]{:S(2)}) collective-permute-start(bf16[32,176,128]{2,1,0:T(8,128)(2,1)} %constant_dynamic-update-slice_fusion), channel_id=1, source_target_pairs={{0,2},{1,33},{2,4},{3,35},{4,6},{5,37},{6,0},{7,39},{8,10},{9,41},... | collective-permute-start | bytes 4325384 | tf_op jit(solution)/shard_map/ppermute | solution.py:315
  60.4 17.4 %collective-permute-start.26 = (bf16[32,80,128]{2,1,0:T(8,128)(2,1)}, bf16[32,80,128]{2,1,0:T(8,128)(2,1)}, u32[]{:S(2)}, u32[]{:S(2)}) collective-permute-start(bf16[32,80,128]{2,1,0:T(8,128)(2,1)} %constant_dynamic-update-slice_fusion.4), channel_id=1, source_target_pairs={{0,8},{1,9},{2,10},{3,11},{4,12},{5,13},{6,14},{7,15},{8,16},{9,17... | collective-permute-start | bytes 1966088 | tf_op jit(solution)/shard_map/ppermute | solution.py:315
  64.1 14.2 %collective-permute-start.23 = (bf16[32,80,128]{2,1,0:T(8,128)(2,1)}, bf16[32,80,128]{2,1,0:T(8,128)(2,1)}, u32[]{:S(2)}, u32[]{:S(2)}) collective-permute-start(bf16[32,80,128]{2,1,0:T(8,128)(2,1)} %constant_dynamic-update-slice_fusion.4), channel_id=1, source_target_pairs={{0,24},{1,25},{2,26},{3,27},{4,28},{5,29},{6,30},{7,31},{8,0},{9,1... | collective-permute-start | bytes 1966088 | tf_op jit(solution)/shard_map/ppermute | solution.py:315
  73.6 31.8 %collective-permute-start.10 = (bf16[32,176,128]{2,1,0:T(8,128)(2,1)}, bf16[32,176,128]{2,1,0:T(8,128)(2,1)S(1)}, u32[]{:S(2)}, u32[]{:S(2)}) collective-permute-start(bf16[32,176,128]{2,1,0:T(8,128)(2,1)} %constant_dynamic-update-slice_fusion), channel_id=1, source_target_pairs={{0,6},{1,97},{2,0},{3,99},{4,2},{5,101},{6,4},{7,103},{8,14},{9,10... | collective-permute-start | bytes 4325384 | tf_op jit(solution)/shard_map/ppermute | solution.py:315
  77.8 23.7 %collective-permute-start.11 = (bf16[16,176,128]{2,1,0:T(8,128)(2,1)S(1)}, bf16[16,176,128]{2,1,0:T(8,128)(2,1)}, u32[]{:S(2)}, u32[]{:S(2)}) collective-permute-start(bf16[16,176,128]{2,1,0:T(8,128)(2,1)S(1)} %constant_dynamic-update-slice_fusion.2), channel_id=1, source_target_pairs={{0,6},{1,97},{2,0},{3,99},{4,2},{5,101},{6,4},{7,103},{8,14},{9,10... | collective-permute-start | bytes 2162696 | tf_op jit(solution)/shard_map/ppermute | solution.py:315
  78.3 26.9 %collective-permute-start.14 = (bf16[16,176,128]{2,1,0:T(8,128)(2,1)S(1)}, bf16[16,176,128]{2,1,0:T(8,128)(2,1)S(1)}, u32[]{:S(2)}, u32[]{:S(2)}) collective-permute-start(bf16[16,176,128]{2,1,0:T(8,128)(2,1)S(1)} %constant_dynamic-update-slice_fusion.2), channel_id=1, source_target_pairs={{0,2},{1,33},{2,4},{3,35},{4,6},{5,37},{6,0},{7,39},{8,10},{9,41},... | collective-permute-start | bytes 2162696 | tf_op jit(solution)/shard_map/ppermute | solution.py:315
  79.9 45.0 %collective-permute-start.29 = (bf16[32,176,128]{2,1,0:T(8,128)(2,1)}, bf16[32,176,128]{2,1,0:T(8,128)(2,1)}, u32[]{:S(2)}, u32[]{:S(2)}) collective-permute-start(bf16[32,176,128]{2,1,0:T(8,128)(2,1)} %collective-permute-done.13.refs_11_.refs_15_), channel_id=1, source_target_pairs={{0,2},{1,33},{2,4},{3,35},{4,6},{5,37},{6,0},{7,39},{8,10},{9,41},... | collective-permute-start | bytes 4325384 | tf_op jit(solution)/shard_map/ppermute | solution.py:315
  101.4 23.5 %collective-permute-start.28 = (bf16[16,176,128]{2,1,0:T(8,128)(2,1)S(1)}, bf16[16,176,128]{2,1,0:T(8,128)(2,1)}, u32[]{:S(2)}, u32[]{:S(2)}) collective-permute-start(bf16[16,176,128]{2,1,0:T(8,128)(2,1)S(1)} %copy-done.10), channel_id=1, source_target_pairs={{0,6},{1,97},{2,0},{3,99},{4,2},{5,101},{6,4},{7,103},{8,14},{9,10... | collective-permute-start | bytes 2162696 | tf_op jit(solution)/shard_map/ppermute | solution.py:315
  105.2 19.7 %collective-permute-start.30 = (bf16[16,176,128]{2,1,0:T(8,128)(2,1)}, bf16[16,176,128]{2,1,0:T(8,128)(2,1)}, u32[]{:S(2)}, u32[]{:S(2)}) collective-permute-start(bf16[16,176,128]{2,1,0:T(8,128)(2,1)} %collective-permute-done.11.refs_9_.refs_10_), channel_id=1, source_target_pairs={{0,6},{1,97},{2,0},{3,99},{4,2},{5,101},{6,4},{7,103},{8,14},{9,10... | collective-permute-start | bytes 2162696 | tf_op jit(solution)/shard_map/ppermute | solution.py:315
  106.1 18.8 %collective-permute-start.32 = (bf16[32,80,128]{2,1,0:T(8,128)(2,1)}, bf16[32,80,128]{2,1,0:T(8,128)(2,1)}, u32[]{:S(2)}, u32[]{:S(2)}) collective-permute-start(bf16[32,80,128]{2,1,0:T(8,128)(2,1)} %collective-permute-done.26.refs_22_.refs_29_), channel_id=1, source_target_pairs={{0,8},{1,9},{2,10},{3,11},{4,12},{5,13},{6,14},{7,15},{8,16},{9,17... | collective-permute-start | bytes 1966088 | tf_op jit(solution)/shard_map/ppermute | solution.py:315
  106.6 18.3 %collective-permute-start.33 = (bf16[16,80,128]{2,1,0:T(8,128)(2,1)S(1)}, bf16[16,80,128]{2,1,0:T(8,128)(2,1)}, u32[]{:S(2)}, u32[]{:S(2)}) collective-permute-start(bf16[16,80,128]{2,1,0:T(8,128)(2,1)S(1)} %copy-done.16), channel_id=1, source_target_pairs={{0,24},{1,25},{2,26},{3,27},{4,28},{5,29},{6,30},{7,31},{8,0},{9,1... | collective-permute-start | bytes 983048 | tf_op jit(solution)/shard_map/ppermute | solution.py:315
  (29 other events, 482.8 us)
where the time goes:
time: 161 us; the launch traced here: 160 us
  waiting for transfers between devices  49.6 us (31%)
  starting transfers between devices  46.4 us (29%)
  Pallas kernels  24.2 us (15%)
  blocking collectives  22.1 us (14%)
  other arithmetic  7.57 us (5%)
  local copies, waits for them, and re-layouts  7.5 us (5%)
  between operations  2.51 us (2%)
    ppermute x32, waiting for transfers between devices, send(): return lax.ppermute(x, AXES, ring_pairs(rings, step))  48.1 us
    ppermute x32, starting transfers between devices, send(): return lax.ppermute(x, AXES, ring_pairs(rings, step))  46.4 us
    pallas_call x2, Pallas kernels, shell_sums(): pl.pallas_call(functools.partial(shell_kernel, held=held, first=done is N...  24.2 us
    all_to_all x1, blocking collectives, body(): lax.all_to_all(partial.reshape(DEVICES, GROUPS_DEV, 128), AXES, 0, 0, til...  22.1 us
  transfers between devices with their start and end apart: 34, of which 12 were waited for; matrix products, arithmetic and copies ran while one was open for 8% of the time, Pallas kernels for 8%

commit v1 on v0

--- a/solution.py
+++ b/solution.py
@@ -45,6 +45,7 @@
 EARLY = tuple(b for b in ALL if b not in (8, 9, 10))
 SPAN = 64
 NOWHERE = 127
+COLUMNS = 80
 
 
 def sine_terms():
@@ -439,8 +440,9 @@
     member = (jnp.arange(GROUPS, dtype=jnp.int32)[:, None] == group[None, :]).astype(jnp.bfloat16)
     partial = jnp.dot(member, parts, preferred_element_type=jnp.float32)
     partial = partial[:, :128] + partial[:, 128:]
-    arrived = lax.all_to_all(partial.reshape(DEVICES, GROUPS_DEV, 128), AXES, 0, 0, tiled=True)
-    own_groups = jnp.sum(arrived, axis=0)
+    partial = partial[:, :COLUMNS].reshape(DEVICES, GROUPS_DEV * COLUMNS)
+    arrived = lax.all_to_all(partial, AXES, 0, 0, tiled=True)
+    own_groups = jnp.sum(arrived, axis=0).reshape(GROUPS_DEV, COLUMNS)
     return own_groups[:, :SHELLS] / (2.0 * own_groups[:, SHELLS : SHELLS + 1] * jnp.asarray(shell_pixels()))
 
 

time: 161 us -> 161 us (level)
  blocking collectives: 22.1 us -> 20 us
    all_to_all x1, blocking collectives: 22.1 us -> 20 us  [body(): arrived = lax.all_to_all(partial, AXES, 0, 0, tiled=True)]
where the time goes in v1:
time: 161 us; the launch traced here: 160 us
  waiting for transfers between devices  49.6 us (31%)
  starting transfers between devices  46.4 us (29%)
  Pallas kernels  24.2 us (15%)
  blocking collectives  20 us (12%)
  local copies, waits for them, and re-layouts  8.47 us (5%)
  other arithmetic  7.67 us (5%)
  between operations  2.53 us (2%)
    ppermute x32, waiting for transfers between devices, send(): return lax.ppermute(x, AXES, ring_pairs(rings, step))  48.1 us
    ppermute x32, starting transfers between devices, send(): return lax.ppermute(x, AXES, ring_pairs(rings, step))  46.4 us
    pallas_call x2, Pallas kernels, shell_sums(): pl.pallas_call(functools.partial(shell_kernel, held=held, first=done is N...  24.2 us
    all_to_all x1, blocking collectives, body(): arrived = lax.all_to_all(partial, AXES, 0, 0, tiled=True)  20 us
  transfers between devices with their start and end apart: 34, of which 12 were waited for; matrix products, arithmetic and copies ran while one was open for 8% of the time, Pallas kernels for 8%

profile of v1, /device:TPU:0, one launch (start us, length us, event | category | flops | bytes accessed | tf_op | source)
XLA Modules:
  0.0 159.6 jit_solution(1075781304283694220)
XLA Ops:
  0.9 2.9 %collective-permute-start.15 = (bf16[4,80,128]{2,1,0:T(8,128)(2,1)S(1)}, bf16[4,80,128]{2,1,0:T(8,128)(2,1)S(1)}, u32[]{:S(2)}, u32[]{:S(2)}) collective-permute-start(bf16[4,80,128]{2,1,0:T(8,128)(2,1)S(1)} %slice.51), channel_id=1, source_target_pairs={{0,6},{1,97},{2,0},{3,99},{4,2},{5,101},{6,4},{7,103},{8,14},{9,10... | collective-permute-start | bytes 245768 | tf_op jit(solution)/shard_map/ppermute | solution.py:316
  6.4 3.1 %collective-permute-start.2 = (bf16[4,176,128]{2,1,0:T(8,128)(2,1)S(1)}, bf16[4,176,128]{2,1,0:T(8,128)(2,1)S(1)}, u32[]{:S(2)}, u32[]{:S(2)}) collective-permute-start(bf16[4,176,128]{2,1,0:T(8,128)(2,1)S(1)} %slice.48), channel_id=1, source_target_pairs={{0,24},{1,7},{2,26},{3,1},{4,28},{5,3},{6,30},{7,5},{8,0},{9,15},{... | collective-permute-start | bytes 540680 | tf_op jit(solution)/shard_map/ppermute | solution.py:316
  12.0 1.5 collective-permute-done
  13.5 2.0 %collective-permute-start.19 = (bf16[16,80,128]{2,1,0:T(8,128)(2,1)S(1)}, bf16[16,80,128]{2,1,0:T(8,128)(2,1)S(1)}, u32[]{:S(2)}, u32[]{:S(2)}) collective-permute-start(bf16[16,80,128]{2,1,0:T(8,128)(2,1)S(1)} %pad_maximum_fusion.1.refs_13_.refs_17_), channel_id=1, source_target_pairs={{0,32},{1,3},{2,34},{3,5},{4,36},{5,7},{6,38},{7,1},{8,40},{9,11},... | collective-permute-start | bytes 983048 | tf_op jit(solution)/shard_map/ppermute | solution.py:316
  16.3 2.2 %collective-permute-start.18 = (bf16[16,80,128]{2,1,0:T(8,128)(2,1)S(1)}, bf16[16,80,128]{2,1,0:T(8,128)(2,1)S(1)}, u32[]{:S(2)}, u32[]{:S(2)}) collective-permute-start(bf16[16,80,128]{2,1,0:T(8,128)(2,1)S(1)} %pad_maximum_fusion.1.refs_13_.refs_17_), channel_id=1, source_target_pairs={{0,96},{1,7},{2,98},{3,1},{4,100},{5,3},{6,102},{7,5},{8,104},{9,1... | collective-permute-start | bytes 983048 | tf_op jit(solution)/shard_map/ppermute | solution.py:316
  18.4 3.0 %collective-permute-start.22 = (bf16[16,80,128]{2,1,0:T(8,128)(2,1)S(1)}, bf16[16,80,128]{2,1,0:T(8,128)(2,1)}, u32[]{:S(2)}, u32[]{:S(2)}) collective-permute-start(bf16[16,80,128]{2,1,0:T(8,128)(2,1)S(1)} %pad_maximum_fusion.1.refs_13_.refs_17_), channel_id=1, source_target_pairs={{0,24},{1,25},{2,26},{3,27},{4,28},{5,29},{6,30},{7,31},{8,0},{9,1... | collective-permute-start | bytes 983048 | tf_op jit(solution)/shard_map/ppermute | solution.py:316
  22.7 2.2 %collective-permute-start.5 = (bf16[16,176,128]{2,1,0:T(8,128)(2,1)S(1)}, bf16[16,176,128]{2,1,0:T(8,128)(2,1)S(1)}, u32[]{:S(2)}, u32[]{:S(2)}) collective-permute-start(bf16[16,176,128]{2,1,0:T(8,128)(2,1)S(1)} %pad_maximum_fusion.refs_2_.refs_3_), channel_id=1, source_target_pairs={{0,96},{1,25},{2,98},{3,27},{4,100},{5,29},{6,102},{7,31},{8,104},... | collective-permute-start | bytes 2162696 | tf_op jit(solution)/shard_map/ppermute | solution.py:316
  25.3 4.2 %collective-permute-done.22.refs_18_.refs_22_ = bf16[16,80,128]{2,1,0:T(8,128)(2,1)} collective-permute-done((bf16[16,80,128]{2,1,0:T(8,128)(2,1)S(1)}, bf16[16,80,128]{2,1,0:T(8,128)(2,1)}, u32[]{:S(2)}, u32[]{:S(2)}) %collective-permute-start.22) | collective-permute-done | bytes 327712 | tf_op jit(solution)/shard_map/ppermute | solution.py:316
  29.6 2.5 %collective-permute-start.21 = (bf16[8,80,128]{2,1,0:T(8,128)(2,1)S(1)}, bf16[8,80,128]{2,1,0:T(8,128)(2,1)S(1)}, u32[]{:S(2)}, u32[]{:S(2)}) collective-permute-start(bf16[8,80,128]{2,1,0:T(8,128)(2,1)S(1)} %slice.53), channel_id=1, source_target_pairs={{0,96},{1,7},{2,98},{3,1},{4,100},{5,3},{6,102},{7,5},{8,104},{9,1... | collective-permute-start | bytes 491528 | tf_op jit(solution)/shard_map/ppermute | solution.py:316
  32.2 3.7 %collective-permute-done.20.refs_16_.refs_20_ = bf16[8,80,128]{2,1,0:T(8,128)(2,1)S(1)} collective-permute-done((bf16[8,80,128]{2,1,0:T(8,128)(2,1)S(1)}, bf16[8,80,128]{2,1,0:T(8,128)(2,1)S(1)}, u32[]{:S(2)}, u32[]{:S(2)}) %collective-permute-start.20) | collective-permute-done | bytes 163872 | tf_op jit(solution)/shard_map/ppermute | solution.py:316
  35.9 3.2 %collective-permute-start.31 = (bf16[16,80,128]{2,1,0:T(8,128)(2,1)}, bf16[16,80,128]{2,1,0:T(8,128)(2,1)}, u32[]{:S(2)}, u32[]{:S(2)}) collective-permute-start(bf16[16,80,128]{2,1,0:T(8,128)(2,1)} %collective-permute-done.22.refs_18_.refs_22_), channel_id=1, source_target_pairs={{0,24},{1,25},{2,26},{3,27},{4,28},{5,29},{6,30},{7,31},{8,0},{9,1... | collective-permute-start | bytes 983048 | tf_op jit(solution)/shard_map/ppermute | solution.py:316
  40.7 4.7 %collective-permute-done.25.refs_21_.refs_28_ = bf16[16,80,128]{2,1,0:T(8,128)(2,1)} collective-permute-done((bf16[16,80,128]{2,1,0:T(8,128)(2,1)S(1)}, bf16[16,80,128]{2,1,0:T(8,128)(2,1)}, u32[]{:S(2)}, u32[]{:S(2)}) %collective-permute-start.25) | collective-permute-done | bytes 327712 | tf_op jit(solution)/shard_map/ppermute | solution.py:316
  47.6 4.0 %collective-permute-start.9 = (bf16[16,176,128]{2,1,0:T(8,128)(2,1)S(1)}, bf16[16,176,128]{2,1,0:T(8,128)(2,1)S(1)}, u32[]{:S(2)}, u32[]{:S(2)}) collective-permute-start(bf16[16,176,128]{2,1,0:T(8,128)(2,1)S(1)} %pad_maximum_fusion.refs_2_.refs_3_), channel_id=1, source_target_pairs={{0,6},{1,97},{2,0},{3,99},{4,2},{5,101},{6,4},{7,103},{8,14},{9,10... | collective-permute-start | bytes 2162696 | tf_op jit(solution)/shard_map/ppermute | solution.py:316
  53.7 4.5 %collective-permute-done.27.refs_23_.refs_30_ = bf16[16,80,128]{2,1,0:T(8,128)(2,1)S(1)} collective-permute-done((bf16[16,80,128]{2,1,0:T(8,128)(2,1)S(1)}, bf16[16,80,128]{2,1,0:T(8,128)(2,1)S(1)}, u32[]{:S(2)}, u32[]{:S(2)}) %collective-permute-start.27) | collective-permute-done | bytes 327712 | tf_op jit(solution)/shard_map/ppermute | solution.py:316
  60.4 3.7 %collective-permute-done.12.refs_10_.refs_14_ = bf16[16,176,128]{2,1,0:T(8,128)(2,1)S(1)} collective-permute-done((bf16[16,176,128]{2,1,0:T(8,128)(2,1)S(1)}, bf16[16,176,128]{2,1,0:T(8,128)(2,1)S(1)}, u32[]{:S(2)}, u32[]{:S(2)}) %collective-permute-start.12) | collective-permute-done | bytes 720928 | tf_op jit(solution)/shard_map/ppermute | solution.py:316
  66.2 2.4 %collective-permute-start.8 = (bf16[8,176,128]{2,1,0:T(8,128)(2,1)S(1)}, bf16[8,176,128]{2,1,0:T(8,128)(2,1)S(1)}, u32[]{:S(2)}, u32[]{:S(2)}) collective-permute-start(bf16[8,176,128]{2,1,0:T(8,128)(2,1)S(1)} %slice.50), channel_id=1, source_target_pairs={{0,96},{1,25},{2,98},{3,27},{4,100},{5,29},{6,102},{7,31},{8,104},... | collective-permute-start | bytes 1081352 | tf_op jit(solution)/shard_map/ppermute | solution.py:316
  70.4 3.2 %collective-permute-done.8.refs_6_.refs_7_ = bf16[8,176,128]{2,1,0:T(8,128)(2,1)S(1)} collective-permute-done((bf16[8,176,128]{2,1,0:T(8,128)(2,1)S(1)}, bf16[8,176,128]{2,1,0:T(8,128)(2,1)S(1)}, u32[]{:S(2)}, u32[]{:S(2)}) %collective-permute-start.8) | collective-permute-done | bytes 360480 | tf_op jit(solution)/shard_map/ppermute | solution.py:316
  73.6 3.4 %collective-permute-start.10 = (bf16[32,176,128]{2,1,0:T(8,128)(2,1)}, bf16[32,176,128]{2,1,0:T(8,128)(2,1)S(1)}, u32[]{:S(2)}, u32[]{:S(2)}) collective-permute-start(bf16[32,176,128]{2,1,0:T(8,128)(2,1)} %constant_dynamic-update-slice_fusion), channel_id=1, source_target_pairs={{0,6},{1,97},{2,0},{3,99},{4,2},{5,101},{6,4},{7,103},{8,14},{9,10... | collective-permute-start | bytes 4325384 | tf_op jit(solution)/shard_map/ppermute | solution.py:316
  80.9 20.5 %collective-permute-done.11.refs_9_.refs_10_ = bf16[16,176,128]{2,1,0:T(8,128)(2,1)} collective-permute-done((bf16[16,176,128]{2,1,0:T(8,128)(2,1)S(1)}, bf16[16,176,128]{2,1,0:T(8,128)(2,1)}, u32[]{:S(2)}, u32[]{:S(2)}) %collective-permute-start.11) | collective-permute-done | bytes 720928 | tf_op jit(solution)/shard_map/ppermute | solution.py:316
  101.4 3.8 %collective-permute-start.28 = (bf16[16,176,128]{2,1,0:T(8,128)(2,1)S(1)}, bf16[16,176,128]{2,1,0:T(8,128)(2,1)}, u32[]{:S(2)}, u32[]{:S(2)}) collective-permute-start(bf16[16,176,128]{2,1,0:T(8,128)(2,1)S(1)} %copy-done.10), channel_id=1, source_target_pairs={{0,6},{1,97},{2,0},{3,99},{4,2},{5,101},{6,4},{7,103},{8,14},{9,10... | collective-permute-start | bytes 2162696 | tf_op jit(solution)/shard_map/ppermute | solution.py:316
  106.6 3.3 %collective-permute-start.33 = (bf16[16,80,128]{2,1,0:T(8,128)(2,1)S(1)}, bf16[16,80,128]{2,1,0:T(8,128)(2,1)}, u32[]{:S(2)}, u32[]{:S(2)}) collective-permute-start(bf16[16,80,128]{2,1,0:T(8,128)(2,1)S(1)} %copy-done.16), channel_id=1, source_target_pairs={{0,24},{1,25},{2,26},{3,27},{4,28},{5,29},{6,30},{7,31},{8,0},{9,1... | collective-permute-start | bytes 983048 | tf_op jit(solution)/shard_map/ppermute | solution.py:316
  111.4 13.5 %shard_map.145.refs_0_ = f32[264,128]{1,0:T(8,128)} custom-call(s32[1104]{0:T(1024)} %concatenate.33.plan_ref, bf16[128,256,128]{2,1,0:T(8,128)(2,1)} %bitcast.25, bf16[128,256,128]{2,1,0:T(8,128)(2,1)} %collective-permute-done.1.refs_1_.refs_2_, bf16[16,176,128]{2,1,0:T(8,128)(2,1)} %copy-done.2, bf16[16,176,128]{2,1,0:T(8,128)(2,1)} %copy-done.1, ...), custom_call_target="tpu_custom_call" | custom-call | tf_op jit(solution)/shard_map/pallas_call | solution.py:283
  125.0 10.7 %shard_map.146 = f32[264,128]{1,0:T(8,128)} custom-call(s32[1104]{0:T(1024)} %concatenate.32.plan_ref, f32[264,128]{1,0:T(8,128)} %shard_map.145.refs_0_, bf16[128,256,128]{2,1,0:T(8,128)(2,1)} %bitcast.26, bf16[128,256,128]{2,1,0:T(8,128)(2,1)} %collective-permute-done.1.refs_1_.refs_2_, bf16[16,176,128]{2,1,0:T(8,128)(2,1)} %copy-done.2, ...), custom_call_target="tpu_custom_call" | custom-call | tf_op jit(solution)/shard_map/pallas_call | solution.py:283
  138.3 20.0 %all_to_all.10 = f32[128,1,640]{2,1,0:T(1,128)S(1)} all-to-all(f32[128,1,640]{2,1,0:T(1,128)S(1)} %all_to_all.8), channel_id=1, replica_groups=mesh['z'=4,'y'=4,'x'=4,'c'=2] {'z','y','x','c'}, dimensions={0} | all-to-all | bytes 655360 | tf_op jit(solution)/shard_map/all_to_all | solution.py:444
  (139 shorter events, 28.5 us)
Async XLA Ops:
  0.0 106.6 %collective-permute-start.1 = (bf16[128,256,128]{2,1,0:T(8,128)(2,1)}, bf16[128,256,128]{2,1,0:T(8,128)(2,1)}, u32[]{:S(2)}, u32[]{:S(2)}) collective-permute-start(bf16[128,256,128]{2,1,0:T(8,128)(2,1)} %bitcast.24), channel_id=1, source_target_pairs={{0,1},{1,0},{2,3},{3,2},{4,5},{5,4},{6,7},{7,6},{8,9},{9,8},{10,11... | collective-permute-start | bytes 25165832 | tf_op jit(solution)/shard_map/ppermute | solution.py:370
  6.4 9.9 %collective-permute-start.2 = (bf16[4,176,128]{2,1,0:T(8,128)(2,1)S(1)}, bf16[4,176,128]{2,1,0:T(8,128)(2,1)S(1)}, u32[]{:S(2)}, u32[]{:S(2)}) collective-permute-start(bf16[4,176,128]{2,1,0:T(8,128)(2,1)S(1)} %slice.48), channel_id=1, source_target_pairs={{0,24},{1,7},{2,26},{3,1},{4,28},{5,3},{6,30},{7,5},{8,0},{9,15},{... | collective-permute-start | bytes 540680 | tf_op jit(solution)/shard_map/ppermute | solution.py:316
  10.9 10.6 %collective-permute-start.4 = (bf16[4,176,128]{2,1,0:T(8,128)(2,1)S(1)}, bf16[4,176,128]{2,1,0:T(8,128)(2,1)S(1)}, u32[]{:S(2)}, u32[]{:S(2)}) collective-permute-start(bf16[4,176,128]{2,1,0:T(8,128)(2,1)S(1)} %slice.48), channel_id=1, source_target_pairs={{0,8},{1,3},{2,10},{3,5},{4,12},{5,7},{6,14},{7,1},{8,16},{9,11},{... | collective-permute-start | bytes 540680 | tf_op jit(solution)/shard_map/ppermute | solution.py:316
  18.4 11.1 %collective-permute-start.22 = (bf16[16,80,128]{2,1,0:T(8,128)(2,1)S(1)}, bf16[16,80,128]{2,1,0:T(8,128)(2,1)}, u32[]{:S(2)}, u32[]{:S(2)}) collective-permute-start(bf16[16,80,128]{2,1,0:T(8,128)(2,1)S(1)} %pad_maximum_fusion.1.refs_13_.refs_17_), channel_id=1, source_target_pairs={{0,24},{1,25},{2,26},{3,27},{4,28},{5,29},{6,30},{7,31},{8,0},{9,1... | collective-permute-start | bytes 983048 | tf_op jit(solution)/shard_map/ppermute | solution.py:316
  21.6 26.0 %collective-permute-start.6 = (bf16[16,176,128]{2,1,0:T(8,128)(2,1)S(1)}, bf16[16,176,128]{2,1,0:T(8,128)(2,1)S(1)}, u32[]{:S(2)}, u32[]{:S(2)}) collective-permute-start(bf16[16,176,128]{2,1,0:T(8,128)(2,1)S(1)} %pad_maximum_fusion.refs_2_.refs_3_), channel_id=1, source_target_pairs={{0,32},{1,9},{2,34},{3,11},{4,36},{5,13},{6,38},{7,15},{8,40},{9,1... | collective-permute-start | bytes 2162696 | tf_op jit(solution)/shard_map/ppermute | solution.py:316
  22.7 28.9 %collective-permute-start.5 = (bf16[16,176,128]{2,1,0:T(8,128)(2,1)S(1)}, bf16[16,176,128]{2,1,0:T(8,128)(2,1)S(1)}, u32[]{:S(2)}, u32[]{:S(2)}) collective-permute-start(bf16[16,176,128]{2,1,0:T(8,128)(2,1)S(1)} %pad_maximum_fusion.refs_2_.refs_3_), channel_id=1, source_target_pairs={{0,96},{1,25},{2,98},{3,27},{4,100},{5,29},{6,102},{7,31},{8,104},... | collective-permute-start | bytes 2162696 | tf_op jit(solution)/shard_map/ppermute | solution.py:316
  25.0 10.9 %collective-permute-start.20 = (bf16[8,80,128]{2,1,0:T(8,128)(2,1)S(1)}, bf16[8,80,128]{2,1,0:T(8,128)(2,1)S(1)}, u32[]{:S(2)}, u32[]{:S(2)}) collective-permute-start(bf16[8,80,128]{2,1,0:T(8,128)(2,1)S(1)} %slice.52), channel_id=1, source_target_pairs={{0,32},{1,3},{2,34},{3,5},{4,36},{5,7},{6,38},{7,1},{8,40},{9,11},... | collective-permute-start | bytes 491528 | tf_op jit(solution)/shard_map/ppermute | solution.py:316
  35.9 9.5 %collective-permute-start.25 = (bf16[16,80,128]{2,1,0:T(8,128)(2,1)S(1)}, bf16[16,80,128]{2,1,0:T(8,128)(2,1)}, u32[]{:S(2)}, u32[]{:S(2)}) collective-permute-start(bf16[16,80,128]{2,1,0:T(8,128)(2,1)S(1)} %pad_maximum_fusion.1.refs_13_.refs_17_), channel_id=1, source_target_pairs={{0,8},{1,9},{2,10},{3,11},{4,12},{5,13},{6,14},{7,15},{8,16},{9,17... | collective-permute-start | bytes 983048 | tf_op jit(solution)/shard_map/ppermute | solution.py:316
  35.9 10.5 %collective-permute-start.31 = (bf16[16,80,128]{2,1,0:T(8,128)(2,1)}, bf16[16,80,128]{2,1,0:T(8,128)(2,1)}, u32[]{:S(2)}, u32[]{:S(2)}) collective-permute-start(bf16[16,80,128]{2,1,0:T(8,128)(2,1)} %collective-permute-done.22.refs_18_.refs_22_), channel_id=1, source_target_pairs={{0,24},{1,25},{2,26},{3,27},{4,28},{5,29},{6,30},{7,31},{8,0},{9,1... | collective-permute-start | bytes 983048 | tf_op jit(solution)/shard_map/ppermute | solution.py:316
  46.4 11.8 %collective-permute-start.27 = (bf16[16,80,128]{2,1,0:T(8,128)(2,1)S(1)}, bf16[16,80,128]{2,1,0:T(8,128)(2,1)S(1)}, u32[]{:S(2)}, u32[]{:S(2)}) collective-permute-start(bf16[16,80,128]{2,1,0:T(8,128)(2,1)S(1)} %constant_dynamic-update-slice_fusion.6), channel_id=1, source_target_pairs={{0,8},{1,9},{2,10},{3,11},{4,12},{5,13},{6,14},{7,15},{8,16},{9,17... | collective-permute-start | bytes 983048 | tf_op jit(solution)/shard_map/ppermute | solution.py:316
  47.6 12.9 %collective-permute-start.9 = (bf16[16,176,128]{2,1,0:T(8,128)(2,1)S(1)}, bf16[16,176,128]{2,1,0:T(8,128)(2,1)S(1)}, u32[]{:S(2)}, u32[]{:S(2)}) collective-permute-start(bf16[16,176,128]{2,1,0:T(8,128)(2,1)S(1)} %pad_maximum_fusion.refs_2_.refs_3_), channel_id=1, source_target_pairs={{0,6},{1,97},{2,0},{3,99},{4,2},{5,101},{6,4},{7,103},{8,14},{9,10... | collective-permute-start | bytes 2162696 | tf_op jit(solution)/shard_map/ppermute | solution.py:316
  51.6 12.5 %collective-permute-start.12 = (bf16[16,176,128]{2,1,0:T(8,128)(2,1)S(1)}, bf16[16,176,128]{2,1,0:T(8,128)(2,1)S(1)}, u32[]{:S(2)}, u32[]{:S(2)}) collective-permute-start(bf16[16,176,128]{2,1,0:T(8,128)(2,1)S(1)} %pad_maximum_fusion.refs_2_.refs_3_), channel_id=1, source_target_pairs={{0,2},{1,33},{2,4},{3,35},{4,6},{5,37},{6,0},{7,39},{8,10},{9,41},... | collective-permute-start | bytes 2162696 | tf_op jit(solution)/shard_map/ppermute | solution.py:316
  53.6 12.6 %collective-permute-start.7 = (bf16[8,176,128]{2,1,0:T(8,128)(2,1)S(1)}, bf16[8,176,128]{2,1,0:T(8,128)(2,1)S(1)}, u32[]{:S(2)}, u32[]{:S(2)}) collective-permute-start(bf16[8,176,128]{2,1,0:T(8,128)(2,1)S(1)} %slice.49), channel_id=1, source_target_pairs={{0,32},{1,9},{2,34},{3,11},{4,36},{5,13},{6,38},{7,15},{8,40},{9,1... | collective-permute-start | bytes 1081352 | tf_op jit(solution)/shard_map/ppermute | solution.py:316
  58.2 21.7 %collective-permute-start.13 = (bf16[32,176,128]{2,1,0:T(8,128)(2,1)}, bf16[32,176,128]{2,1,0:T(8,128)(2,1)}, u32[]{:S(2)}, u32[]{:S(2)}) collective-permute-start(bf16[32,176,128]{2,1,0:T(8,128)(2,1)} %constant_dynamic-update-slice_fusion), channel_id=1, source_target_pairs={{0,2},{1,33},{2,4},{3,35},{4,6},{5,37},{6,0},{7,39},{8,10},{9,41},... | collective-permute-start | bytes 4325384 | tf_op jit(solution)/shard_map/ppermute | solution.py:316
  60.4 17.4 %collective-permute-start.26 = (bf16[32,80,128]{2,1,0:T(8,128)(2,1)}, bf16[32,80,128]{2,1,0:T(8,128)(2,1)}, u32[]{:S(2)}, u32[]{:S(2)}) collective-permute-start(bf16[32,80,128]{2,1,0:T(8,128)(2,1)} %constant_dynamic-update-slice_fusion.4), channel_id=1, source_target_pairs={{0,8},{1,9},{2,10},{3,11},{4,12},{5,13},{6,14},{7,15},{8,16},{9,17... | collective-permute-start | bytes 1966088 | tf_op jit(solution)/shard_map/ppermute | solution.py:316
  64.1 14.2 %collective-permute-start.23 = (bf16[32,80,128]{2,1,0:T(8,128)(2,1)}, bf16[32,80,128]{2,1,0:T(8,128)(2,1)}, u32[]{:S(2)}, u32[]{:S(2)}) collective-permute-start(bf16[32,80,128]{2,1,0:T(8,128)(2,1)} %constant_dynamic-update-slice_fusion.4), channel_id=1, source_target_pairs={{0,24},{1,25},{2,26},{3,27},{4,28},{5,29},{6,30},{7,31},{8,0},{9,1... | collective-permute-start | bytes 1966088 | tf_op jit(solution)/shard_map/ppermute | solution.py:316
  73.6 31.8 %collective-permute-start.10 = (bf16[32,176,128]{2,1,0:T(8,128)(2,1)}, bf16[32,176,128]{2,1,0:T(8,128)(2,1)S(1)}, u32[]{:S(2)}, u32[]{:S(2)}) collective-permute-start(bf16[32,176,128]{2,1,0:T(8,128)(2,1)} %constant_dynamic-update-slice_fusion), channel_id=1, source_target_pairs={{0,6},{1,97},{2,0},{3,99},{4,2},{5,101},{6,4},{7,103},{8,14},{9,10... | collective-permute-start | bytes 4325384 | tf_op jit(solution)/shard_map/ppermute | solution.py:316
  77.8 23.7 %collective-permute-start.11 = (bf16[16,176,128]{2,1,0:T(8,128)(2,1)S(1)}, bf16[16,176,128]{2,1,0:T(8,128)(2,1)}, u32[]{:S(2)}, u32[]{:S(2)}) collective-permute-start(bf16[16,176,128]{2,1,0:T(8,128)(2,1)S(1)} %constant_dynamic-update-slice_fusion.2), channel_id=1, source_target_pairs={{0,6},{1,97},{2,0},{3,99},{4,2},{5,101},{6,4},{7,103},{8,14},{9,10... | collective-permute-start | bytes 2162696 | tf_op jit(solution)/shard_map/ppermute | solution.py:316
  78.3 26.9 %collective-permute-start.14 = (bf16[16,176,128]{2,1,0:T(8,128)(2,1)S(1)}, bf16[16,176,128]{2,1,0:T(8,128)(2,1)S(1)}, u32[]{:S(2)}, u32[]{:S(2)}) collective-permute-start(bf16[16,176,128]{2,1,0:T(8,128)(2,1)S(1)} %constant_dynamic-update-slice_fusion.2), channel_id=1, source_target_pairs={{0,2},{1,33},{2,4},{3,35},{4,6},{5,37},{6,0},{7,39},{8,10},{9,41},... | collective-permute-start | bytes 2162696 | tf_op jit(solution)/shard_map/ppermute | solution.py:316
  79.9 45.0 %collective-permute-start.29 = (bf16[32,176,128]{2,1,0:T(8,128)(2,1)}, bf16[32,176,128]{2,1,0:T(8,128)(2,1)}, u32[]{:S(2)}, u32[]{:S(2)}) collective-permute-start(bf16[32,176,128]{2,1,0:T(8,128)(2,1)} %collective-permute-done.13.refs_11_.refs_15_), channel_id=1, source_target_pairs={{0,2},{1,33},{2,4},{3,35},{4,6},{5,37},{6,0},{7,39},{8,10},{9,41},... | collective-permute-start | bytes 4325384 | tf_op jit(solution)/shard_map/ppermute | solution.py:316
  101.4 23.5 %collective-permute-start.28 = (bf16[16,176,128]{2,1,0:T(8,128)(2,1)S(1)}, bf16[16,176,128]{2,1,0:T(8,128)(2,1)}, u32[]{:S(2)}, u32[]{:S(2)}) collective-permute-start(bf16[16,176,128]{2,1,0:T(8,128)(2,1)S(1)} %copy-done.10), channel_id=1, source_target_pairs={{0,6},{1,97},{2,0},{3,99},{4,2},{5,101},{6,4},{7,103},{8,14},{9,10... | collective-permute-start | bytes 2162696 | tf_op jit(solution)/shard_map/ppermute | solution.py:316
  105.2 19.7 %collective-permute-start.30 = (bf16[16,176,128]{2,1,0:T(8,128)(2,1)}, bf16[16,176,128]{2,1,0:T(8,128)(2,1)}, u32[]{:S(2)}, u32[]{:S(2)}) collective-permute-start(bf16[16,176,128]{2,1,0:T(8,128)(2,1)} %collective-permute-done.11.refs_9_.refs_10_), channel_id=1, source_target_pairs={{0,6},{1,97},{2,0},{3,99},{4,2},{5,101},{6,4},{7,103},{8,14},{9,10... | collective-permute-start | bytes 2162696 | tf_op jit(solution)/shard_map/ppermute | solution.py:316
  106.1 18.8 %collective-permute-start.32 = (bf16[32,80,128]{2,1,0:T(8,128)(2,1)}, bf16[32,80,128]{2,1,0:T(8,128)(2,1)}, u32[]{:S(2)}, u32[]{:S(2)}) collective-permute-start(bf16[32,80,128]{2,1,0:T(8,128)(2,1)} %collective-permute-done.26.refs_22_.refs_29_), channel_id=1, source_target_pairs={{0,8},{1,9},{2,10},{3,11},{4,12},{5,13},{6,14},{7,15},{8,16},{9,17... | collective-permute-start | bytes 1966088 | tf_op jit(solution)/shard_map/ppermute | solution.py:316
  106.6 18.3 %collective-permute-start.33 = (bf16[16,80,128]{2,1,0:T(8,128)(2,1)S(1)}, bf16[16,80,128]{2,1,0:T(8,128)(2,1)}, u32[]{:S(2)}, u32[]{:S(2)}) collective-permute-start(bf16[16,80,128]{2,1,0:T(8,128)(2,1)S(1)} %copy-done.16), channel_id=1, source_target_pairs={{0,24},{1,25},{2,26},{3,27},{4,28},{5,29},{6,30},{7,31},{8,0},{9,1... | collective-permute-start | bytes 983048 | tf_op jit(solution)/shard_map/ppermute | solution.py:316
  (29 other events, 481.6 us)

commit v2 on v1

--- a/solution.py
+++ b/solution.py
@@ -128,13 +128,14 @@
                     fetch(low + 4 * i + k)
                 return carry
 
-            def fetch_one(t, carry, fetch=fetch):
-                fetch(t)
-                return carry
-
             fours = (high - low) // 4
             lax.fori_loop(0, fours, fetch_some, 0)
-            lax.fori_loop(low + 4 * fours, high, fetch_one, 0)
+            for k in range(3):
+                left_over = low + 4 * fours + k
+
+                @pl.when(left_over < high)
+                def _(fetch=fetch, left_over=left_over):
+                    fetch(left_over)
 
     def start(j, slot):
         at = plan_ref[IMAGE_AT + j]

time: 161 us -> 161 us (level)
  transfers between devices with their start and end apart: 34 -> 34, of which waited for: 12 -> 12; matrix products, arithmetic and copies ran while one was open for 8% -> 8% of each run, Pallas kernels for 8% -> 9%
where the time goes in v2:
time: 161 us; the launch traced here: 160 us
  waiting for transfers between devices  49.6 us (31%)
  starting transfers between devices  46.4 us (29%)
  Pallas kernels  24.8 us (15%)
  blocking collectives  20 us (12%)
  local copies, waits for them, and re-layouts  8.47 us (5%)
  other arithmetic  7.67 us (5%)
  between operations  2.53 us (2%)
    ppermute x32, waiting for transfers between devices, send(): return lax.ppermute(x, AXES, ring_pairs(rings, step))  48.1 us
    ppermute x32, starting transfers between devices, send(): return lax.ppermute(x, AXES, ring_pairs(rings, step))  46.4 us
    pallas_call x2, Pallas kernels, shell_sums(): pl.pallas_call(functools.partial(shell_kernel, held=held, first=done is N...  24.8 us
    all_to_all x1, blocking collectives, body(): arrived = lax.all_to_all(partial, AXES, 0, 0, tiled=True)  20 us
  transfers between devices with their start and end apart: 34, of which 12 were waited for; matrix products, arithmetic and copies ran while one was open for 8% of the time, Pallas kernels for 9%

profile of v2, /device:TPU:0, one launch (start us, length us, event | category | flops | bytes accessed | tf_op | source)
XLA Modules:
  0.0 160.1 jit_solution(638322555601949590)
XLA Ops:
  0.9 2.9 %collective-permute-start.15 = (bf16[4,80,128]{2,1,0:T(8,128)(2,1)S(1)}, bf16[4,80,128]{2,1,0:T(8,128)(2,1)S(1)}, u32[]{:S(2)}, u32[]{:S(2)}) collective-permute-start(bf16[4,80,128]{2,1,0:T(8,128)(2,1)S(1)} %slice.51), channel_id=1, source_target_pairs={{0,6},{1,97},{2,0},{3,99},{4,2},{5,101},{6,4},{7,103},{8,14},{9,10... | collective-permute-start | bytes 245768 | tf_op jit(solution)/shard_map/ppermute | solution.py:317
  6.4 3.1 %collective-permute-start.2 = (bf16[4,176,128]{2,1,0:T(8,128)(2,1)S(1)}, bf16[4,176,128]{2,1,0:T(8,128)(2,1)S(1)}, u32[]{:S(2)}, u32[]{:S(2)}) collective-permute-start(bf16[4,176,128]{2,1,0:T(8,128)(2,1)S(1)} %slice.48), channel_id=1, source_target_pairs={{0,24},{1,7},{2,26},{3,1},{4,28},{5,3},{6,30},{7,5},{8,0},{9,15},{... | collective-permute-start | bytes 540680 | tf_op jit(solution)/shard_map/ppermute | solution.py:317
  12.0 1.5 collective-permute-done
  13.5 2.0 %collective-permute-start.19 = (bf16[16,80,128]{2,1,0:T(8,128)(2,1)S(1)}, bf16[16,80,128]{2,1,0:T(8,128)(2,1)S(1)}, u32[]{:S(2)}, u32[]{:S(2)}) collective-permute-start(bf16[16,80,128]{2,1,0:T(8,128)(2,1)S(1)} %pad_maximum_fusion.1.refs_13_.refs_17_), channel_id=1, source_target_pairs={{0,32},{1,3},{2,34},{3,5},{4,36},{5,7},{6,38},{7,1},{8,40},{9,11},... | collective-permute-start | bytes 983048 | tf_op jit(solution)/shard_map/ppermute | solution.py:317
  16.3 2.2 %collective-permute-start.18 = (bf16[16,80,128]{2,1,0:T(8,128)(2,1)S(1)}, bf16[16,80,128]{2,1,0:T(8,128)(2,1)S(1)}, u32[]{:S(2)}, u32[]{:S(2)}) collective-permute-start(bf16[16,80,128]{2,1,0:T(8,128)(2,1)S(1)} %pad_maximum_fusion.1.refs_13_.refs_17_), channel_id=1, source_target_pairs={{0,96},{1,7},{2,98},{3,1},{4,100},{5,3},{6,102},{7,5},{8,104},{9,1... | collective-permute-start | bytes 983048 | tf_op jit(solution)/shard_map/ppermute | solution.py:317
  18.4 3.0 %collective-permute-start.22 = (bf16[16,80,128]{2,1,0:T(8,128)(2,1)S(1)}, bf16[16,80,128]{2,1,0:T(8,128)(2,1)}, u32[]{:S(2)}, u32[]{:S(2)}) collective-permute-start(bf16[16,80,128]{2,1,0:T(8,128)(2,1)S(1)} %pad_maximum_fusion.1.refs_13_.refs_17_), channel_id=1, source_target_pairs={{0,24},{1,25},{2,26},{3,27},{4,28},{5,29},{6,30},{7,31},{8,0},{9,1... | collective-permute-start | bytes 983048 | tf_op jit(solution)/shard_map/ppermute | solution.py:317
  22.7 2.2 %collective-permute-start.5 = (bf16[16,176,128]{2,1,0:T(8,128)(2,1)S(1)}, bf16[16,176,128]{2,1,0:T(8,128)(2,1)S(1)}, u32[]{:S(2)}, u32[]{:S(2)}) collective-permute-start(bf16[16,176,128]{2,1,0:T(8,128)(2,1)S(1)} %pad_maximum_fusion.refs_2_.refs_3_), channel_id=1, source_target_pairs={{0,96},{1,25},{2,98},{3,27},{4,100},{5,29},{6,102},{7,31},{8,104},... | collective-permute-start | bytes 2162696 | tf_op jit(solution)/shard_map/ppermute | solution.py:317
  25.3 4.2 %collective-permute-done.22.refs_18_.refs_22_ = bf16[16,80,128]{2,1,0:T(8,128)(2,1)} collective-permute-done((bf16[16,80,128]{2,1,0:T(8,128)(2,1)S(1)}, bf16[16,80,128]{2,1,0:T(8,128)(2,1)}, u32[]{:S(2)}, u32[]{:S(2)}) %collective-permute-start.22) | collective-permute-done | bytes 327712 | tf_op jit(solution)/shard_map/ppermute | solution.py:317
  29.6 2.5 %collective-permute-start.21 = (bf16[8,80,128]{2,1,0:T(8,128)(2,1)S(1)}, bf16[8,80,128]{2,1,0:T(8,128)(2,1)S(1)}, u32[]{:S(2)}, u32[]{:S(2)}) collective-permute-start(bf16[8,80,128]{2,1,0:T(8,128)(2,1)S(1)} %slice.53), channel_id=1, source_target_pairs={{0,96},{1,7},{2,98},{3,1},{4,100},{5,3},{6,102},{7,5},{8,104},{9,1... | collective-permute-start | bytes 491528 | tf_op jit(solution)/shard_map/ppermute | solution.py:317
  32.2 3.7 %collective-permute-done.20.refs_16_.refs_20_ = bf16[8,80,128]{2,1,0:T(8,128)(2,1)S(1)} collective-permute-done((bf16[8,80,128]{2,1,0:T(8,128)(2,1)S(1)}, bf16[8,80,128]{2,1,0:T(8,128)(2,1)S(1)}, u32[]{:S(2)}, u32[]{:S(2)}) %collective-permute-start.20) | collective-permute-done | bytes 163872 | tf_op jit(solution)/shard_map/ppermute | solution.py:317
  35.9 3.2 %collective-permute-start.31 = (bf16[16,80,128]{2,1,0:T(8,128)(2,1)}, bf16[16,80,128]{2,1,0:T(8,128)(2,1)}, u32[]{:S(2)}, u32[]{:S(2)}) collective-permute-start(bf16[16,80,128]{2,1,0:T(8,128)(2,1)} %collective-permute-done.22.refs_18_.refs_22_), channel_id=1, source_target_pairs={{0,24},{1,25},{2,26},{3,27},{4,28},{5,29},{6,30},{7,31},{8,0},{9,1... | collective-permute-start | bytes 983048 | tf_op jit(solution)/shard_map/ppermute | solution.py:317
  40.7 4.7 %collective-permute-done.25.refs_21_.refs_28_ = bf16[16,80,128]{2,1,0:T(8,128)(2,1)} collective-permute-done((bf16[16,80,128]{2,1,0:T(8,128)(2,1)S(1)}, bf16[16,80,128]{2,1,0:T(8,128)(2,1)}, u32[]{:S(2)}, u32[]{:S(2)}) %collective-permute-start.25) | collective-permute-done | bytes 327712 | tf_op jit(solution)/shard_map/ppermute | solution.py:317
  47.6 4.0 %collective-permute-start.9 = (bf16[16,176,128]{2,1,0:T(8,128)(2,1)S(1)}, bf16[16,176,128]{2,1,0:T(8,128)(2,1)S(1)}, u32[]{:S(2)}, u32[]{:S(2)}) collective-permute-start(bf16[16,176,128]{2,1,0:T(8,128)(2,1)S(1)} %pad_maximum_fusion.refs_2_.refs_3_), channel_id=1, source_target_pairs={{0,6},{1,97},{2,0},{3,99},{4,2},{5,101},{6,4},{7,103},{8,14},{9,10... | collective-permute-start | bytes 2162696 | tf_op jit(solution)/shard_map/ppermute | solution.py:317
  53.7 4.5 %collective-permute-done.27.refs_23_.refs_30_ = bf16[16,80,128]{2,1,0:T(8,128)(2,1)S(1)} collective-permute-done((bf16[16,80,128]{2,1,0:T(8,128)(2,1)S(1)}, bf16[16,80,128]{2,1,0:T(8,128)(2,1)S(1)}, u32[]{:S(2)}, u32[]{:S(2)}) %collective-permute-start.27) | collective-permute-done | bytes 327712 | tf_op jit(solution)/shard_map/ppermute | solution.py:317
  60.4 3.7 %collective-permute-done.12.refs_10_.refs_14_ = bf16[16,176,128]{2,1,0:T(8,128)(2,1)S(1)} collective-permute-done((bf16[16,176,128]{2,1,0:T(8,128)(2,1)S(1)}, bf16[16,176,128]{2,1,0:T(8,128)(2,1)S(1)}, u32[]{:S(2)}, u32[]{:S(2)}) %collective-permute-start.12) | collective-permute-done | bytes 720928 | tf_op jit(solution)/shard_map/ppermute | solution.py:317
  66.2 2.4 %collective-permute-start.8 = (bf16[8,176,128]{2,1,0:T(8,128)(2,1)S(1)}, bf16[8,176,128]{2,1,0:T(8,128)(2,1)S(1)}, u32[]{:S(2)}, u32[]{:S(2)}) collective-permute-start(bf16[8,176,128]{2,1,0:T(8,128)(2,1)S(1)} %slice.50), channel_id=1, source_target_pairs={{0,96},{1,25},{2,98},{3,27},{4,100},{5,29},{6,102},{7,31},{8,104},... | collective-permute-start | bytes 1081352 | tf_op jit(solution)/shard_map/ppermute | solution.py:317
  70.4 3.2 %collective-permute-done.8.refs_6_.refs_7_ = bf16[8,176,128]{2,1,0:T(8,128)(2,1)S(1)} collective-permute-done((bf16[8,176,128]{2,1,0:T(8,128)(2,1)S(1)}, bf16[8,176,128]{2,1,0:T(8,128)(2,1)S(1)}, u32[]{:S(2)}, u32[]{:S(2)}) %collective-permute-start.8) | collective-permute-done | bytes 360480 | tf_op jit(solution)/shard_map/ppermute | solution.py:317
  73.6 3.4 %collective-permute-start.10 = (bf16[32,176,128]{2,1,0:T(8,128)(2,1)}, bf16[32,176,128]{2,1,0:T(8,128)(2,1)S(1)}, u32[]{:S(2)}, u32[]{:S(2)}) collective-permute-start(bf16[32,176,128]{2,1,0:T(8,128)(2,1)} %constant_dynamic-update-slice_fusion), channel_id=1, source_target_pairs={{0,6},{1,97},{2,0},{3,99},{4,2},{5,101},{6,4},{7,103},{8,14},{9,10... | collective-permute-start | bytes 4325384 | tf_op jit(solution)/shard_map/ppermute | solution.py:317
  80.9 20.5 %collective-permute-done.11.refs_9_.refs_10_ = bf16[16,176,128]{2,1,0:T(8,128)(2,1)} collective-permute-done((bf16[16,176,128]{2,1,0:T(8,128)(2,1)S(1)}, bf16[16,176,128]{2,1,0:T(8,128)(2,1)}, u32[]{:S(2)}, u32[]{:S(2)}) %collective-permute-start.11) | collective-permute-done | bytes 720928 | tf_op jit(solution)/shard_map/ppermute | solution.py:317
  101.4 3.8 %collective-permute-start.28 = (bf16[16,176,128]{2,1,0:T(8,128)(2,1)S(1)}, bf16[16,176,128]{2,1,0:T(8,128)(2,1)}, u32[]{:S(2)}, u32[]{:S(2)}) collective-permute-start(bf16[16,176,128]{2,1,0:T(8,128)(2,1)S(1)} %copy-done.10), channel_id=1, source_target_pairs={{0,6},{1,97},{2,0},{3,99},{4,2},{5,101},{6,4},{7,103},{8,14},{9,10... | collective-permute-start | bytes 2162696 | tf_op jit(solution)/shard_map/ppermute | solution.py:317
  106.6 3.3 %collective-permute-start.33 = (bf16[16,80,128]{2,1,0:T(8,128)(2,1)S(1)}, bf16[16,80,128]{2,1,0:T(8,128)(2,1)}, u32[]{:S(2)}, u32[]{:S(2)}) collective-permute-start(bf16[16,80,128]{2,1,0:T(8,128)(2,1)S(1)} %copy-done.16), channel_id=1, source_target_pairs={{0,24},{1,25},{2,26},{3,27},{4,28},{5,29},{6,30},{7,31},{8,0},{9,1... | collective-permute-start | bytes 983048 | tf_op jit(solution)/shard_map/ppermute | solution.py:317
  111.4 13.7 %shard_map.145.refs_0_ = f32[264,128]{1,0:T(8,128)} custom-call(s32[1104]{0:T(1024)} %concatenate.33.plan_ref, bf16[128,256,128]{2,1,0:T(8,128)(2,1)} %bitcast.25, bf16[128,256,128]{2,1,0:T(8,128)(2,1)} %collective-permute-done.1.refs_1_.refs_2_, bf16[16,176,128]{2,1,0:T(8,128)(2,1)} %copy-done.2, bf16[16,176,128]{2,1,0:T(8,128)(2,1)} %copy-done.1, ...), custom_call_target="tpu_custom_call" | custom-call | tf_op jit(solution)/shard_map/pallas_call | solution.py:284
  125.2 11.1 %shard_map.146 = f32[264,128]{1,0:T(8,128)} custom-call(s32[1104]{0:T(1024)} %concatenate.32.plan_ref, f32[264,128]{1,0:T(8,128)} %shard_map.145.refs_0_, bf16[128,256,128]{2,1,0:T(8,128)(2,1)} %bitcast.26, bf16[128,256,128]{2,1,0:T(8,128)(2,1)} %collective-permute-done.1.refs_1_.refs_2_, bf16[16,176,128]{2,1,0:T(8,128)(2,1)} %copy-done.2, ...), custom_call_target="tpu_custom_call" | custom-call | tf_op jit(solution)/shard_map/pallas_call | solution.py:284
  138.8 20.0 %all_to_all.10 = f32[128,1,640]{2,1,0:T(1,128)S(1)} all-to-all(f32[128,1,640]{2,1,0:T(1,128)S(1)} %all_to_all.8), channel_id=1, replica_groups=mesh['z'=4,'y'=4,'x'=4,'c'=2] {'z','y','x','c'}, dimensions={0} | all-to-all | bytes 655360 | tf_op jit(solution)/shard_map/all_to_all | solution.py:445
  (139 shorter events, 28.5 us)
Async XLA Ops:
  0.0 106.6 %collective-permute-start.1 = (bf16[128,256,128]{2,1,0:T(8,128)(2,1)}, bf16[128,256,128]{2,1,0:T(8,128)(2,1)}, u32[]{:S(2)}, u32[]{:S(2)}) collective-permute-start(bf16[128,256,128]{2,1,0:T(8,128)(2,1)} %bitcast.24), channel_id=1, source_target_pairs={{0,1},{1,0},{2,3},{3,2},{4,5},{5,4},{6,7},{7,6},{8,9},{9,8},{10,11... | collective-permute-start | bytes 25165832 | tf_op jit(solution)/shard_map/ppermute | solution.py:371
  6.4 9.9 %collective-permute-start.2 = (bf16[4,176,128]{2,1,0:T(8,128)(2,1)S(1)}, bf16[4,176,128]{2,1,0:T(8,128)(2,1)S(1)}, u32[]{:S(2)}, u32[]{:S(2)}) collective-permute-start(bf16[4,176,128]{2,1,0:T(8,128)(2,1)S(1)} %slice.48), channel_id=1, source_target_pairs={{0,24},{1,7},{2,26},{3,1},{4,28},{5,3},{6,30},{7,5},{8,0},{9,15},{... | collective-permute-start | bytes 540680 | tf_op jit(solution)/shard_map/ppermute | solution.py:317
  10.9 10.6 %collective-permute-start.4 = (bf16[4,176,128]{2,1,0:T(8,128)(2,1)S(1)}, bf16[4,176,128]{2,1,0:T(8,128)(2,1)S(1)}, u32[]{:S(2)}, u32[]{:S(2)}) collective-permute-start(bf16[4,176,128]{2,1,0:T(8,128)(2,1)S(1)} %slice.48), channel_id=1, source_target_pairs={{0,8},{1,3},{2,10},{3,5},{4,12},{5,7},{6,14},{7,1},{8,16},{9,11},{... | collective-permute-start | bytes 540680 | tf_op jit(solution)/shard_map/ppermute | solution.py:317
  18.4 11.1 %collective-permute-start.22 = (bf16[16,80,128]{2,1,0:T(8,128)(2,1)S(1)}, bf16[16,80,128]{2,1,0:T(8,128)(2,1)}, u32[]{:S(2)}, u32[]{:S(2)}) collective-permute-start(bf16[16,80,128]{2,1,0:T(8,128)(2,1)S(1)} %pad_maximum_fusion.1.refs_13_.refs_17_), channel_id=1, source_target_pairs={{0,24},{1,25},{2,26},{3,27},{4,28},{5,29},{6,30},{7,31},{8,0},{9,1... | collective-permute-start | bytes 983048 | tf_op jit(solution)/shard_map/ppermute | solution.py:317
  21.6 26.0 %collective-permute-start.6 = (bf16[16,176,128]{2,1,0:T(8,128)(2,1)S(1)}, bf16[16,176,128]{2,1,0:T(8,128)(2,1)S(1)}, u32[]{:S(2)}, u32[]{:S(2)}) collective-permute-start(bf16[16,176,128]{2,1,0:T(8,128)(2,1)S(1)} %pad_maximum_fusion.refs_2_.refs_3_), channel_id=1, source_target_pairs={{0,32},{1,9},{2,34},{3,11},{4,36},{5,13},{6,38},{7,15},{8,40},{9,1... | collective-permute-start | bytes 2162696 | tf_op jit(solution)/shard_map/ppermute | solution.py:317
  22.7 28.9 %collective-permute-start.5 = (bf16[16,176,128]{2,1,0:T(8,128)(2,1)S(1)}, bf16[16,176,128]{2,1,0:T(8,128)(2,1)S(1)}, u32[]{:S(2)}, u32[]{:S(2)}) collective-permute-start(bf16[16,176,128]{2,1,0:T(8,128)(2,1)S(1)} %pad_maximum_fusion.refs_2_.refs_3_), channel_id=1, source_target_pairs={{0,96},{1,25},{2,98},{3,27},{4,100},{5,29},{6,102},{7,31},{8,104},... | collective-permute-start | bytes 2162696 | tf_op jit(solution)/shard_map/ppermute | solution.py:317
  25.0 10.9 %collective-permute-start.20 = (bf16[8,80,128]{2,1,0:T(8,128)(2,1)S(1)}, bf16[8,80,128]{2,1,0:T(8,128)(2,1)S(1)}, u32[]{:S(2)}, u32[]{:S(2)}) collective-permute-start(bf16[8,80,128]{2,1,0:T(8,128)(2,1)S(1)} %slice.52), channel_id=1, source_target_pairs={{0,32},{1,3},{2,34},{3,5},{4,36},{5,7},{6,38},{7,1},{8,40},{9,11},... | collective-permute-start | bytes 491528 | tf_op jit(solution)/shard_map/ppermute | solution.py:317
  35.9 9.5 %collective-permute-start.25 = (bf16[16,80,128]{2,1,0:T(8,128)(2,1)S(1)}, bf16[16,80,128]{2,1,0:T(8,128)(2,1)}, u32[]{:S(2)}, u32[]{:S(2)}) collective-permute-start(bf16[16,80,128]{2,1,0:T(8,128)(2,1)S(1)} %pad_maximum_fusion.1.refs_13_.refs_17_), channel_id=1, source_target_pairs={{0,8},{1,9},{2,10},{3,11},{4,12},{5,13},{6,14},{7,15},{8,16},{9,17... | collective-permute-start | bytes 983048 | tf_op jit(solution)/shard_map/ppermute | solution.py:317
  35.9 10.5 %collective-permute-start.31 = (bf16[16,80,128]{2,1,0:T(8,128)(2,1)}, bf16[16,80,128]{2,1,0:T(8,128)(2,1)}, u32[]{:S(2)}, u32[]{:S(2)}) collective-permute-start(bf16[16,80,128]{2,1,0:T(8,128)(2,1)} %collective-permute-done.22.refs_18_.refs_22_), channel_id=1, source_target_pairs={{0,24},{1,25},{2,26},{3,27},{4,28},{5,29},{6,30},{7,31},{8,0},{9,1... | collective-permute-start | bytes 983048 | tf_op jit(solution)/shard_map/ppermute | solution.py:317
  46.4 11.8 %collective-permute-start.27 = (bf16[16,80,128]{2,1,0:T(8,128)(2,1)S(1)}, bf16[16,80,128]{2,1,0:T(8,128)(2,1)S(1)}, u32[]{:S(2)}, u32[]{:S(2)}) collective-permute-start(bf16[16,80,128]{2,1,0:T(8,128)(2,1)S(1)} %constant_dynamic-update-slice_fusion.6), channel_id=1, source_target_pairs={{0,8},{1,9},{2,10},{3,11},{4,12},{5,13},{6,14},{7,15},{8,16},{9,17... | collective-permute-start | bytes 983048 | tf_op jit(solution)/shard_map/ppermute | solution.py:317
  47.6 12.9 %collective-permute-start.9 = (bf16[16,176,128]{2,1,0:T(8,128)(2,1)S(1)}, bf16[16,176,128]{2,1,0:T(8,128)(2,1)S(1)}, u32[]{:S(2)}, u32[]{:S(2)}) collective-permute-start(bf16[16,176,128]{2,1,0:T(8,128)(2,1)S(1)} %pad_maximum_fusion.refs_2_.refs_3_), channel_id=1, source_target_pairs={{0,6},{1,97},{2,0},{3,99},{4,2},{5,101},{6,4},{7,103},{8,14},{9,10... | collective-permute-start | bytes 2162696 | tf_op jit(solution)/shard_map/ppermute | solution.py:317
  51.6 12.5 %collective-permute-start.12 = (bf16[16,176,128]{2,1,0:T(8,128)(2,1)S(1)}, bf16[16,176,128]{2,1,0:T(8,128)(2,1)S(1)}, u32[]{:S(2)}, u32[]{:S(2)}) collective-permute-start(bf16[16,176,128]{2,1,0:T(8,128)(2,1)S(1)} %pad_maximum_fusion.refs_2_.refs_3_), channel_id=1, source_target_pairs={{0,2},{1,33},{2,4},{3,35},{4,6},{5,37},{6,0},{7,39},{8,10},{9,41},... | collective-permute-start | bytes 2162696 | tf_op jit(solution)/shard_map/ppermute | solution.py:317
  53.6 12.6 %collective-permute-start.7 = (bf16[8,176,128]{2,1,0:T(8,128)(2,1)S(1)}, bf16[8,176,128]{2,1,0:T(8,128)(2,1)S(1)}, u32[]{:S(2)}, u32[]{:S(2)}) collective-permute-start(bf16[8,176,128]{2,1,0:T(8,128)(2,1)S(1)} %slice.49), channel_id=1, source_target_pairs={{0,32},{1,9},{2,34},{3,11},{4,36},{5,13},{6,38},{7,15},{8,40},{9,1... | collective-permute-start | bytes 1081352 | tf_op jit(solution)/shard_map/ppermute | solution.py:317
  58.2 21.7 %collective-permute-start.13 = (bf16[32,176,128]{2,1,0:T(8,128)(2,1)}, bf16[32,176,128]{2,1,0:T(8,128)(2,1)}, u32[]{:S(2)}, u32[]{:S(2)}) collective-permute-start(bf16[32,176,128]{2,1,0:T(8,128)(2,1)} %constant_dynamic-update-slice_fusion), channel_id=1, source_target_pairs={{0,2},{1,33},{2,4},{3,35},{4,6},{5,37},{6,0},{7,39},{8,10},{9,41},... | collective-permute-start | bytes 4325384 | tf_op jit(solution)/shard_map/ppermute | solution.py:317
  60.4 17.4 %collective-permute-start.26 = (bf16[32,80,128]{2,1,0:T(8,128)(2,1)}, bf16[32,80,128]{2,1,0:T(8,128)(2,1)}, u32[]{:S(2)}, u32[]{:S(2)}) collective-permute-start(bf16[32,80,128]{2,1,0:T(8,128)(2,1)} %constant_dynamic-update-slice_fusion.4), channel_id=1, source_target_pairs={{0,8},{1,9},{2,10},{3,11},{4,12},{5,13},{6,14},{7,15},{8,16},{9,17... | collective-permute-start | bytes 1966088 | tf_op jit(solution)/shard_map/ppermute | solution.py:317
  64.1 14.2 %collective-permute-start.23 = (bf16[32,80,128]{2,1,0:T(8,128)(2,1)}, bf16[32,80,128]{2,1,0:T(8,128)(2,1)}, u32[]{:S(2)}, u32[]{:S(2)}) collective-permute-start(bf16[32,80,128]{2,1,0:T(8,128)(2,1)} %constant_dynamic-update-slice_fusion.4), channel_id=1, source_target_pairs={{0,24},{1,25},{2,26},{3,27},{4,28},{5,29},{6,30},{7,31},{8,0},{9,1... | collective-permute-start | bytes 1966088 | tf_op jit(solution)/shard_map/ppermute | solution.py:317
  73.6 31.8 %collective-permute-start.10 = (bf16[32,176,128]{2,1,0:T(8,128)(2,1)}, bf16[32,176,128]{2,1,0:T(8,128)(2,1)S(1)}, u32[]{:S(2)}, u32[]{:S(2)}) collective-permute-start(bf16[32,176,128]{2,1,0:T(8,128)(2,1)} %constant_dynamic-update-slice_fusion), channel_id=1, source_target_pairs={{0,6},{1,97},{2,0},{3,99},{4,2},{5,101},{6,4},{7,103},{8,14},{9,10... | collective-permute-start | bytes 4325384 | tf_op jit(solution)/shard_map/ppermute | solution.py:317
  77.8 23.7 %collective-permute-start.11 = (bf16[16,176,128]{2,1,0:T(8,128)(2,1)S(1)}, bf16[16,176,128]{2,1,0:T(8,128)(2,1)}, u32[]{:S(2)}, u32[]{:S(2)}) collective-permute-start(bf16[16,176,128]{2,1,0:T(8,128)(2,1)S(1)} %constant_dynamic-update-slice_fusion.2), channel_id=1, source_target_pairs={{0,6},{1,97},{2,0},{3,99},{4,2},{5,101},{6,4},{7,103},{8,14},{9,10... | collective-permute-start | bytes 2162696 | tf_op jit(solution)/shard_map/ppermute | solution.py:317
  78.3 26.9 %collective-permute-start.14 = (bf16[16,176,128]{2,1,0:T(8,128)(2,1)S(1)}, bf16[16,176,128]{2,1,0:T(8,128)(2,1)S(1)}, u32[]{:S(2)}, u32[]{:S(2)}) collective-permute-start(bf16[16,176,128]{2,1,0:T(8,128)(2,1)S(1)} %constant_dynamic-update-slice_fusion.2), channel_id=1, source_target_pairs={{0,2},{1,33},{2,4},{3,35},{4,6},{5,37},{6,0},{7,39},{8,10},{9,41},... | collective-permute-start | bytes 2162696 | tf_op jit(solution)/shard_map/ppermute | solution.py:317
  79.9 45.2 %collective-permute-start.29 = (bf16[32,176,128]{2,1,0:T(8,128)(2,1)}, bf16[32,176,128]{2,1,0:T(8,128)(2,1)}, u32[]{:S(2)}, u32[]{:S(2)}) collective-permute-start(bf16[32,176,128]{2,1,0:T(8,128)(2,1)} %collective-permute-done.13.refs_11_.refs_15_), channel_id=1, source_target_pairs={{0,2},{1,33},{2,4},{3,35},{4,6},{5,37},{6,0},{7,39},{8,10},{9,41},... | collective-permute-start | bytes 4325384 | tf_op jit(solution)/shard_map/ppermute | solution.py:317
  101.4 23.7 %collective-permute-start.28 = (bf16[16,176,128]{2,1,0:T(8,128)(2,1)S(1)}, bf16[16,176,128]{2,1,0:T(8,128)(2,1)}, u32[]{:S(2)}, u32[]{:S(2)}) collective-permute-start(bf16[16,176,128]{2,1,0:T(8,128)(2,1)S(1)} %copy-done.10), channel_id=1, source_target_pairs={{0,6},{1,97},{2,0},{3,99},{4,2},{5,101},{6,4},{7,103},{8,14},{9,10... | collective-permute-start | bytes 2162696 | tf_op jit(solution)/shard_map/ppermute | solution.py:317
  105.2 19.9 %collective-permute-start.30 = (bf16[16,176,128]{2,1,0:T(8,128)(2,1)}, bf16[16,176,128]{2,1,0:T(8,128)(2,1)}, u32[]{:S(2)}, u32[]{:S(2)}) collective-permute-start(bf16[16,176,128]{2,1,0:T(8,128)(2,1)} %collective-permute-done.11.refs_9_.refs_10_), channel_id=1, source_target_pairs={{0,6},{1,97},{2,0},{3,99},{4,2},{5,101},{6,4},{7,103},{8,14},{9,10... | collective-permute-start | bytes 2162696 | tf_op jit(solution)/shard_map/ppermute | solution.py:317
  106.1 19.0 %collective-permute-start.32 = (bf16[32,80,128]{2,1,0:T(8,128)(2,1)}, bf16[32,80,128]{2,1,0:T(8,128)(2,1)}, u32[]{:S(2)}, u32[]{:S(2)}) collective-permute-start(bf16[32,80,128]{2,1,0:T(8,128)(2,1)} %collective-permute-done.26.refs_22_.refs_29_), channel_id=1, source_target_pairs={{0,8},{1,9},{2,10},{3,11},{4,12},{5,13},{6,14},{7,15},{8,16},{9,17... | collective-permute-start | bytes 1966088 | tf_op jit(solution)/shard_map/ppermute | solution.py:317
  106.6 18.5 %collective-permute-start.33 = (bf16[16,80,128]{2,1,0:T(8,128)(2,1)S(1)}, bf16[16,80,128]{2,1,0:T(8,128)(2,1)}, u32[]{:S(2)}, u32[]{:S(2)}) collective-permute-start(bf16[16,80,128]{2,1,0:T(8,128)(2,1)S(1)} %copy-done.16), channel_id=1, source_target_pairs={{0,24},{1,25},{2,26},{3,27},{4,28},{5,29},{6,30},{7,31},{8,0},{9,1... | collective-permute-start | bytes 983048 | tf_op jit(solution)/shard_map/ppermute | solution.py:317
  (29 other events, 481.6 us)
